TPU v7x, 768 devices: a whole 4x8x12 slice. The times are simulated.
768 devices in a mesh: region: 16 (over y, core), sub: 48 (over x, z).
Axes of the slice: x: 4, y: 8, z: 12, core: 2. Of those that a mesh axis runs over, the one named last changes fastest.
Arguments:
- coords: float32 [3, 49152, 128], P(None, ('region', 'sub')), may hold values from -3 to 3
- smooth: float32 [49152, 128], P(('region', 'sub')), may hold values from 0.6 to 1.5
- masses: float32 [49152, 128], P(('region', 'sub')), may hold values from 0.01 to 0.1
- owners: int32 [49152], P(('region', 'sub')), may hold values from 0 to 15, as said below
- counts: int32 [49152], P(('region', 'sub')), may hold values from 32 to 128
- neighbours: int32 [49152, 4], P(('region', 'sub')), may hold values from 0 to 71, as said below
Outputs:
- density: float32 [49152, 128], P(('region', 'sub'))
- accel: float32 [3, 49152, 128], P(None, ('region', 'sub'))
Inputs may be any that keep to these rules, and one draw needn't show every extreme that they name: `owners`: within the 64 tiles of each device's block, every value 0 to 16 - 1 appears exactly 4 times. `neighbours`: the first entry of the list of slot t is 4 + t (the tile itself); the entries of one list are distinct and lie within 4 of 4 + t.
All inputs are finite; a program needn't handle non-finite values.
Results may differ from a plain program's by a relative error of at most 0.0001.
Values sent between devices are 32-bit elements; how exact they have to be, the bound alone decides.
A program may use at most 64 MiB of HBM per device.

v0:
```python
import math

import jax
import jax.numpy as jnp
from jax import lax
from jax.sharding import PartitionSpec as P

HALO_TILES = 4


kernel_scale = math.pi ** (-1.5)


def extended_2(x, sides, width):
    for axis, dim in sides:
        devices, length = (lax.axis_size(axis), x.shape[dim])
        up = [(i, (i + 1) % devices) for i in range(devices)]
        down = [(j, i) for i, j in up]
        last = lax.slice_in_dim(x, length - width, length, axis=dim)
        initial = lax.slice_in_dim(x, 0, width, axis=dim)
        before = lax.ppermute(last, axis, up)
        after = lax.ppermute(initial, axis, down)
        x = jnp.concatenate([before, x, after], axis=dim)
    return x


def pair_weights(pos_own, inverse_sq, kernel_norm, pos_partner):
    offset_vec = pos_own[:, :, :, None] - pos_partner[:, :, None, :]
    distance_sq = jnp.sum(offset_vec * offset_vec, axis=0)
    return (offset_vec, jnp.exp(-distance_sq * inverse_sq[:, :, None]) * kernel_norm[:, :, None])


def tile_terms(own_tiles):
    smooth_len = own_tiles[3]
    inverse_sq = 1.0 / (smooth_len * smooth_len)
    kernel_norm = kernel_scale * inverse_sq / smooth_len
    return (inverse_sq, kernel_norm)


def density_core(own_tiles, source, lists):
    inverse_sq, kernel_norm = tile_terms(own_tiles)
    partners = jnp.take(source, lists, axis=1)
    density = jnp.zeros(inverse_sq.shape, jnp.float32)
    for nb_slot in range(lists.shape[1]):
        partner = partners[:, :, nb_slot]
        unused, weight_pair = pair_weights(own_tiles[:3], inverse_sq, kernel_norm, partner[:3])
        density = density + jnp.sum(weight_pair * partner[4][:, None, :], axis=-1)
    return density


def force_pass(extended, pressure_ext, neighbours, pressure_own):
    tile_dev = neighbours.shape[0]
    own_tiles = extended[:, HALO_TILES : HALO_TILES + tile_dev]
    inverse_sq, kernel_norm = tile_terms(own_tiles)
    partners = jnp.take(extended, neighbours, axis=1)
    pressure_nb = jnp.take(pressure_ext, neighbours, axis=0)
    accel_sum = jnp.zeros((3,) + inverse_sq.shape, jnp.float32)
    for nb_slot in range(neighbours.shape[1]):
        partner = partners[:, :, nb_slot]
        offset_vec, weight_pair = pair_weights(own_tiles[:3], inverse_sq, kernel_norm, partner[:3])
        coefficient = (
            weight_pair
            * partner[4][:, None, :]
            * (pressure_own[:, :, None] + pressure_nb[:, nb_slot][:, None, :])
        )
        accel_sum = accel_sum + jnp.sum(offset_vec * coefficient[None], axis=-1)
    return 2.0 * inverse_sq[None] * accel_sum


def pressure_of(raw_density, live_mask):
    safe_density = jnp.where(live_mask > 0, raw_density, 1.0)
    return jnp.where(live_mask > 0, safe_density ** (-1.0 / 3.0), 0.0)


def per_device(coords, smooth, masses, owners, counts, neighbours):
    tile_dev, tile_rows = smooth.shape
    regions = lax.axis_size("region")
    per_dest = tile_dev // regions
    fields = jnp.concatenate([coords, smooth[None], masses[None]], axis=0)
    ordering = jnp.argsort(owners, stable=True)
    grouped = jnp.take(fields, ordering, axis=1).reshape(5, regions, per_dest, tile_rows)
    arrived = lax.all_to_all(grouped, "region", split_axis=1, concat_axis=1, tiled=True).reshape(
        5, tile_dev, tile_rows
    )
    slot_ids = jnp.arange(tile_rows, dtype=jnp.int32)
    live_mask = (slot_ids[None, :] < counts[:, None]).astype(jnp.float32)
    outgoing = jnp.concatenate([arrived[:4], (arrived[4] * live_mask)[None]], axis=0)
    extended = extended_2(outgoing, (("sub", 1),), HALO_TILES)
    own_tiles = extended[:, HALO_TILES : HALO_TILES + tile_dev]
    raw_density = density_core(own_tiles, extended, neighbours)
    pressure_own = pressure_of(raw_density, live_mask)
    pressure_ext = extended_2(pressure_own, (("sub", 0),), HALO_TILES)
    accel = force_pass(extended, pressure_ext, neighbours, pressure_own)
    return (raw_density * live_mask, accel * live_mask[None])


def solution(mesh):
    in_specs = (
        P(None, ("region", "sub"), None),
        P(("region", "sub"), None),
        P(("region", "sub"), None),
        P(("region", "sub")),
        P(("region", "sub")),
        P(("region", "sub"), None),
    )
    out_specs = (P(("region", "sub"), None), P(None, ("region", "sub"), None))
    return jax.shard_map(
        per_device, mesh=mesh, in_specs=in_specs, out_specs=out_specs, check_vma=False
    )
```

profile of v0, /device:TPU:1, one launch (start us, length us, event | category | flops | bytes accessed | tf_op | source)
XLA Modules:
  0.0 119.9 jit_solution(2668421214992995289)
XLA Ops:
  0.6 2.7 %sort.17 = (s32[64]{0:T(128)}, s32[64]{0:T(128)S(1)}) sort(s32[64]{0:T(128)} %param.11, s32[64]{0:T(128)S(1)} %iota.21), dimensions={0}, to_apply=%region_0.0 | sort | flops 384 | bytes 1024 | tf_op jit(solution)/shard_map/jit(argsort)/sort | solution.py:80
  3.3 1.0 copy.43
  4.3 0.1 broadcast_in_dim.42
  4.4 0.9 pad_maximum_fusion.1
  5.3 0.6 gather_fusion
  5.9 0.8 copy_select_fusion
  6.7 13.8 %all-to-all-start = ((f32[5,16,4,128]{3,2,0,1:T(4,128)}), f32[5,16,4,128]{3,2,0,1:T(4,128)S(1)}, u32[]{:S(2)}, u32[]{:S(2)}) async-start(f32[5,16,4,128]{3,2,0,1:T(4,128)} %copy_select_fusion), calls=%async_computation | async-start | bytes 327680 | tf_op jit(solution)/shard_map/all_to_all | solution.py:82
  20.5 0.7 compare_select_fusion.1
  21.1 0.7 compare_and_fusion
  21.8 0.1 copy.48
  21.9 0.1 reshape.226
  22.0 0.1 copy.46
  22.2 0.7 fusion.12
  22.9 7.2 %all-to-all-done = f32[5,16,4,128]{3,2,0,1:T(4,128)S(1)} async-done(((f32[5,16,4,128]{3,2,0,1:T(4,128)}), f32[5,16,4,128]{3,2,0,1:T(4,128)S(1)}, u32[]{:S(2)}, u32[]{:S(2)}) %all-to-all-start) | async-done | bytes 163872 | tf_op jit(solution)/shard_map/all_to_all | solution.py:82
  30.1 0.8 compare_select_fusion
  31.0 11.2 %collective-permute-start.1 = (f32[5,4,128]{2,0,1:T(8,128)S(1)}, f32[5,4,128]{2,0,1:T(8,128)S(1)}, u32[]{:S(2)}, u32[]{:S(2)}) collective-permute-start(f32[5,4,128]{2,0,1:T(8,128)S(1)} %get-tuple-element.30), channel_id=1, source_target_pairs={{1,0},{2,1},{3,2},{4,3},{5,4},{6,5},{7,6},{8,7},{9,8},{10,9},{11,1... | collective-permute-start | bytes 30728 | tf_op jit(solution)/shard_map/ppermute | solution.py:22
  42.2 1.9 %collective-permute-start = (f32[5,4,128]{2,0,1:T(8,128)S(1)}, f32[5,4,128]{2,0,1:T(8,128)S(1)}, u32[]{:S(2)}, u32[]{:S(2)}) collective-permute-start(f32[5,4,128]{2,0,1:T(8,128)S(1)} %get-tuple-element.29), channel_id=1, source_target_pairs={{0,1},{1,2},{2,3},{3,4},{4,5},{5,6},{6,7},{7,8},{8,9},{9,10},{10,1... | collective-permute-start | bytes 30728 | tf_op jit(solution)/shard_map/ppermute | solution.py:21
  44.2 0.0 collective-permute-done.1
  44.2 5.8 %collective-permute-done = f32[5,4,128]{2,0,1:T(8,128)S(1)} collective-permute-done((f32[5,4,128]{2,0,1:T(8,128)S(1)}, f32[5,4,128]{2,0,1:T(8,128)S(1)}, u32[]{:S(2)}, u32[]{:S(2)}) %collective-permute-start) | collective-permute-done | bytes 10272 | tf_op jit(solution)/shard_map/ppermute | solution.py:21
  50.0 0.1 pad_maximum_fusion
  50.1 1.0 gather_fusion.2
  51.1 0.3 select_bitcast_fusion
  51.5 0.1 slice_bitcast_fusion.3
  51.6 0.1 fusion.14
  51.8 16.2 %fusion.2 = (f32[64,128,128]{2,1,0:T(8,128)S(1)}, f32[64,128,128]{2,1,0:T(8,128)}, f32[64,128,128]{2,1,0:T(8,128)}, f32[64,128,128]{2,1,0:T(8,128)}) fusion(f32[3,64,128]{2,1,0:T(8,128)S(1)} %copy.50, f32[3,64,128]{2,1,0:T(8,128)S(1)} %bitcast.32, f32[3,64,128]{2,1,0:T(8,128)S(1)} %copy.51, f32[3,64,128]{2,1,0:T(8,128)S(1)} %copy.52, f32[3,64,128]{2,1,0:T(8,128)S(1)} %copy.49), kind=kLoop, calls=%fused_computation.13 | loop fusion | flops 33554432 | bytes 17268736 | tf_op jit(solution)/shard_map/reduce_sum | solution.py:29
  68.0 0.0 copy-start
  68.0 0.0 copy-start.1
  68.0 12.1 %fusion.9 = (f32[64,128]{1,0:T(8,128)S(1)}, f32[64,128]{1,0:T(8,128)S(1)}, f32[64,128]{1,0:T(8,128)S(1)}, f32[64,128]{1,0:T(8,128)S(1)}) fusion(f32[64,128,128]{2,1,0:T(8,128)S(1)} %get-tuple-element.9, f32[64,128]{1,0:T(8,128)S(1)} %bitcast.42, f32[64,128]{1,0:T(8,128)S(1)} %get-tuple-element.40, f32[64,128]{1,0:T(8,128)S(1)} %get-tuple-element.41, ...), kind=kLoop, calls=%fused_computation.28 | loop fusion | flops 20938752 | bytes 17104896 | tf_op jit(solution)/shard_map/reduce_sum | solution.py:47
  80.0 0.0 copy-done
  80.0 0.0 copy-done.1
  80.1 0.1 power_select_fusion
  80.2 1.9 %collective-permute-start.3 = (f32[4,128]{1,0:T(4,128)S(1)}, f32[4,128]{1,0:T(4,128)S(1)}, u32[]{:S(2)}, u32[]{:S(2)}) collective-permute-start(f32[4,128]{1,0:T(4,128)S(1)} %get-tuple-element.43), channel_id=1, source_target_pairs={{1,0},{2,1},{3,2},{4,3},{5,4},{6,5},{7,6},{8,7},{9,8},{10,9},{11,1... | collective-permute-start | bytes 6152 | tf_op jit(solution)/shard_map/ppermute | solution.py:22
  82.1 3.4 %collective-permute-start.2 = (f32[4,128]{1,0:T(4,128)S(1)}, f32[4,128]{1,0:T(4,128)S(1)}, u32[]{:S(2)}, u32[]{:S(2)}) collective-permute-start(f32[4,128]{1,0:T(4,128)S(1)} %get-tuple-element.42), channel_id=1, source_target_pairs={{0,1},{1,2},{2,3},{3,4},{4,5},{5,6},{6,7},{7,8},{8,9},{9,10},{10,1... | collective-permute-start | bytes 6152 | tf_op jit(solution)/shard_map/ppermute | solution.py:21
  85.5 0.7 fusion.13
  86.2 0.0 collective-permute-done.3
  86.2 3.6 %collective-permute-done.2 = f32[4,128]{1,0:T(4,128)S(1)} collective-permute-done((f32[4,128]{1,0:T(4,128)S(1)}, f32[4,128]{1,0:T(4,128)S(1)}, u32[]{:S(2)}, u32[]{:S(2)}) %collective-permute-start.2) | collective-permute-done | bytes 2080 | tf_op jit(solution)/shard_map/ppermute | solution.py:21
  89.8 0.7 gather_fusion.1
  90.5 0.1 broadcast_select_fusion
  90.7 0.1 fusion.16
  90.8 7.9 %add_multiply_fusion.3 = (f32[64,128,128]{2,1,0:T(8,128)S(1)}, f32[64,128,128]{2,1,0:T(8,128)S(1)}, f32[64,128,128]{2,1,0:T(8,128)S(1)}, f32[64,128,128]{2,1,0:T(8,128)S(1)}) fusion(f32[64,128,128]{2,1,0:T(8,128)} %get-tuple-element.12, f32[64,128]{1,0:T(8,128)S(1)} %bitcast.44, f32[64,128]{1,0:T(8,128)S(1)} %get-tuple-element.17, ...), kind=kLoop, calls=%fused_computation.22 | loop fusion | flops 25165824 | bytes 33914880 | tf_op jit(solution)/shard_map/mul | solution.py:62
  98.6 20.6 %fusion.3 = (f32[3,64,128]{2,1,0:T(8,128)S(1)}, f32[3,64,128]{2,1,0:T(8,128)S(1)}, f32[3,64,128]{2,1,0:T(8,128)S(1)}, f32[3,64,128]{2,1,0:T(8,128)S(1)}) fusion(f32[64,128,128]{2,1,0:T(8,128)S(1)} %get-tuple-element.36, f32[3,64,128]{2,1,0:T(8,128)S(1)} %copy.50, f32[3,64,128]{2,1,0:T(8,128)S(1)} %bitcast.33, f32[64,128,128]{2,1,0:T(8,128)S(1)} %get-tuple-element.38, ...), kind=kLoop, calls=%fused_computation.14 | loop fusion | flops 37650432 | bytes 17661952 | tf_op jit(solution)/shard_map/reduce_sum | solution.py:66
  119.2 0.7 multiply_multiply_fusion.4
  (18 shorter events, 0.2 us)
Async XLA Ops:
  6.7 23.4 %all-to-all-start = ((f32[5,16,4,128]{3,2,0,1:T(4,128)}), f32[5,16,4,128]{3,2,0,1:T(4,128)S(1)}, u32[]{:S(2)}, u32[]{:S(2)}) async-start(f32[5,16,4,128]{3,2,0,1:T(4,128)} %copy_select_fusion), calls=%async_computation | async-start | bytes 327680 | tf_op jit(solution)/shard_map/all_to_all | solution.py:82
  31.0 13.2 %collective-permute-start.1 = (f32[5,4,128]{2,0,1:T(8,128)S(1)}, f32[5,4,128]{2,0,1:T(8,128)S(1)}, u32[]{:S(2)}, u32[]{:S(2)}) collective-permute-start(f32[5,4,128]{2,0,1:T(8,128)S(1)} %get-tuple-element.30), channel_id=1, source_target_pairs={{1,0},{2,1},{3,2},{4,3},{5,4},{6,5},{7,6},{8,7},{9,8},{10,9},{11,1... | collective-permute-start | bytes 30728 | tf_op jit(solution)/shard_map/ppermute | solution.py:22
  42.2 7.8 %collective-permute-start = (f32[5,4,128]{2,0,1:T(8,128)S(1)}, f32[5,4,128]{2,0,1:T(8,128)S(1)}, u32[]{:S(2)}, u32[]{:S(2)}) collective-permute-start(f32[5,4,128]{2,0,1:T(8,128)S(1)} %get-tuple-element.29), channel_id=1, source_target_pairs={{0,1},{1,2},{2,3},{3,4},{4,5},{5,6},{6,7},{7,8},{8,9},{9,10},{10,1... | collective-permute-start | bytes 30728 | tf_op jit(solution)/shard_map/ppermute | solution.py:21
  68.0 12.1 %copy-start = (f32[64,128,128]{2,1,0:T(8,128)}, f32[64,128,128]{2,1,0:T(8,128)S(1)}, u32[]{:S(2)}) copy-start(f32[64,128,128]{2,1,0:T(8,128)S(1)} %get-tuple-element.9) | copy-start | bytes 12582916
  68.0 12.1 %copy-start.1 = (s32[64]{0:T(128)S(1)}, s32[64]{0:T(128)}, u32[]{:S(2)}) copy-start(s32[64]{0:T(128)} %param.12) | copy-start | bytes 772
  80.2 6.0 %collective-permute-start.3 = (f32[4,128]{1,0:T(4,128)S(1)}, f32[4,128]{1,0:T(4,128)S(1)}, u32[]{:S(2)}, u32[]{:S(2)}) collective-permute-start(f32[4,128]{1,0:T(4,128)S(1)} %get-tuple-element.43), channel_id=1, source_target_pairs={{1,0},{2,1},{3,2},{4,3},{5,4},{6,5},{7,6},{8,7},{9,8},{10,9},{11,1... | collective-permute-start | bytes 6152 | tf_op jit(solution)/shard_map/ppermute | solution.py:22
  82.1 7.6 %collective-permute-start.2 = (f32[4,128]{1,0:T(4,128)S(1)}, f32[4,128]{1,0:T(4,128)S(1)}, u32[]{:S(2)}, u32[]{:S(2)}) collective-permute-start(f32[4,128]{1,0:T(4,128)S(1)} %get-tuple-element.42), channel_id=1, source_target_pairs={{0,1},{1,2},{2,3},{3,4},{4,5},{5,6},{6,7},{7,8},{8,9},{9,10},{10,1... | collective-permute-start | bytes 6152 | tf_op jit(solution)/shard_map/ppermute | solution.py:21
where the time goes:
time: 120 us
  other arithmetic  66 us (55%)
  starting transfers between devices  32.2 us (27%)
  waiting for transfers between devices  16.6 us (14%)
  local copies, waits for them, and re-layouts  4.22 us (4%)
    reduce_sum x1, other arithmetic, force_pass(): accel_sum = accel_sum + jnp.sum(offset_vec * coefficient[None], axis=-1)  20.6 us
    reduce_sum x1, other arithmetic, pair_weights(): distance_sq = jnp.sum(offset_vec * offset_vec, axis=0)  16.2 us
    all_to_all x1, starting transfers between devices, per_device(): lax.all_to_all(grouped, 'region', split_axis=1, concat_axis=1, tiled=True)  13.8 us
    ppermute x2, starting transfers between devices, extended_2(): after = lax.ppermute(initial, axis, down)  13.2 us
    reduce_sum x1, other arithmetic, density_core(): density = density + jnp.sum(weight_pair * partner[4][:, None, :], axis=-1)  12.1 us
    ppermute x2, waiting for transfers between devices, extended_2(): before = lax.ppermute(last, axis, up)  9.38 us
    mul x1, other arithmetic, force_pass(): weight_pair * partner[4][:, None, :]  7.85 us
    all_to_all x1, waiting for transfers between devices, per_device(): lax.all_to_all(grouped, 'region', split_axis=1, concat_axis=1, tiled=True)  7.19 us
  transfers between devices with their start and end apart: 5, of which 3 were waited for; matrix products, arithmetic and copies ran while one was open for 3% of the time, Pallas kernels for 0%

commit v1 on v0

v1 whole, which is shorter than its diff:
```python
import functools
import math

import jax
import jax.numpy as jnp
from jax import lax
from jax.experimental import pallas as pl
from jax.experimental.pallas import tpu as pltpu
from jax.sharding import PartitionSpec as P

HALO = 4
FIELDS = 5
LOG2E = math.log2(math.e)
NORM_LOG2 = -1.5 * math.log2(math.pi)
DEAD_LOG2 = -1000.0
MESH = pl.DeviceIdType.MESH
F32 = jnp.float32
BF16 = jnp.bfloat16


def split3(v):
    hi = v.astype(BF16).astype(F32)
    rest = v - hi
    mid = rest.astype(BF16).astype(F32)
    return hi, mid, rest - mid


def relayout_kernel(regions, subs, coords_ref, smooth_ref, masses_ref, owners_ref, meta_ref,
                    fields_ref, meta_out_ref, packed, landed, meta_land,
                    send_sem, recv_sem, rim_send, rim_recv, meta_send, meta_recv):
    tile_dev = smooth_ref.shape[0]
    group = tile_dev // regions
    rim = 2 * HALO // group
    r = lax.axis_index("region")
    s = lax.axis_index("sub")
    up = lax.rem(s + 1, subs)
    down = lax.rem(s + subs - 1, subs)

    barrier = pltpu.get_barrier_semaphore()
    for off in range(1, regions):
        pl.semaphore_signal(barrier, inc=1, device_id=(lax.rem(r + off, regions), s), device_id_type=MESH)
    for peer in (up, down):
        pl.semaphore_signal(barrier, inc=1, device_id=(r, peer), device_id_type=MESH)

    own = owners_ref[...]
    hot = (lax.broadcasted_iota(jnp.int32, (regions, tile_dev), 0) == own).astype(F32)
    before = (lax.broadcasted_iota(jnp.int32, (tile_dev, tile_dev), 0)
              < lax.broadcasted_iota(jnp.int32, (tile_dev, tile_dev), 1)).astype(F32)
    count = jnp.dot(hot.astype(BF16), before.astype(BF16), preferred_element_type=F32)
    rank = jnp.sum(hot * count, axis=0, keepdims=True).astype(jnp.int32)
    place = own * 8 + rank
    pick = (lax.broadcasted_iota(jnp.int32, (8 * regions, tile_dev), 0) == place).astype(F32)
    pick3 = jnp.concatenate([pick, pick, pick], axis=1).astype(BF16)
    for f in range(FIELDS):
        field = coords_ref[f] if f < 3 else (smooth_ref[...] if f == 3 else masses_ref[...])
        stack = jnp.concatenate(split3(field), axis=0).astype(BF16)
        got = jnp.dot(pick3, stack, preferred_element_type=F32)
        for d in range(regions):
            packed[d, pl.ds(f, group, stride=FIELDS), :] = got[8 * d : 8 * d + group]

    pl.semaphore_wait(barrier, regions - 1 + 2)

    def meta_copy(slot, peer):
        return pltpu.make_async_remote_copy(
            src_ref=meta_ref, dst_ref=meta_land.at[slot], send_sem=meta_send.at[slot],
            recv_sem=meta_recv.at[slot], device_id=(r, peer), device_id_type=MESH)

    metas = [meta_copy(0, up), meta_copy(1, down)]
    offsets = sorted(range(1, regions), key=lambda o: -min(o, regions - o))
    copies = []
    for off in offsets:
        dst = lax.rem(r + off, regions)
        copies.append(pltpu.make_async_remote_copy(
            src_ref=packed.at[dst], dst_ref=landed.at[rim + r], send_sem=send_sem.at[off],
            recv_sem=recv_sem.at[r], device_id=(dst, s), device_id_type=MESH))
    for copy in copies:
        copy.start()
    for copy in metas:
        copy.start()
    landed[rim + r] = packed[r]

    def arrived(src):
        @pl.when(src != r)
        def _():
            pltpu.make_async_remote_copy(
                src_ref=packed.at[src], dst_ref=landed.at[rim + src], send_sem=send_sem.at[0],
                recv_sem=recv_sem.at[src], device_id=(src, s), device_id_type=MESH).wait_recv()

    first, last = list(range(rim)), list(range(regions - rim, regions))
    for src in first + [g for g in last if g not in first]:
        arrived(src)
    rims = [
        pltpu.make_async_remote_copy(
            src_ref=landed.at[pl.ds(rim, rim)], dst_ref=landed.at[pl.ds(rim + regions, rim)],
            send_sem=rim_send.at[0], recv_sem=rim_recv.at[0], device_id=(r, down), device_id_type=MESH),
        pltpu.make_async_remote_copy(
            src_ref=landed.at[pl.ds(regions, rim)], dst_ref=landed.at[pl.ds(0, rim)],
            send_sem=rim_send.at[1], recv_sem=rim_recv.at[1], device_id=(r, up), device_id_type=MESH),
    ]
    for copy in rims:
        copy.start()
    for src in range(regions):
        if src not in first + last:
            arrived(src)

    def unpack(groups):
        for g in groups:
            for f in range(FIELDS):
                fields_ref[f, group * g : group * (g + 1), :] = landed[g, pl.ds(f, group, stride=FIELDS), :]

    unpack(range(rim, rim + regions))
    for copy in metas:
        copy.wait_recv()
    meta_out_ref[...] = meta_land[...]
    for copy in rims:
        copy.wait_recv()
    unpack(list(range(rim)) + list(range(rim + regions, 2 * rim + regions)))
    for copy in copies + metas + rims:
        copy.wait_send()


def relayout(coords, smooth, masses, owners, meta):
    regions, subs = lax.axis_size("region"), lax.axis_size("sub")
    tile_dev, rows = smooth.shape
    group = tile_dev // regions
    groups = regions + 2 * (2 * HALO // group)
    vmem = pl.BlockSpec(memory_space=pltpu.VMEM)
    return pl.pallas_call(
        functools.partial(relayout_kernel, regions, subs),
        out_shape=(jax.ShapeDtypeStruct((FIELDS, groups * group, rows), F32),
                   jax.ShapeDtypeStruct((2,) + meta.shape, jnp.int32)),
        in_specs=[vmem] * 5,
        out_specs=(vmem, vmem),
        scratch_shapes=[
            pltpu.VMEM((regions, group * FIELDS, rows), F32),
            pltpu.VMEM((groups, group * FIELDS, rows), F32),
            pltpu.VMEM((2,) + meta.shape, jnp.int32),
            pltpu.SemaphoreType.DMA((regions,)),
            pltpu.SemaphoreType.DMA((regions,)),
            pltpu.SemaphoreType.DMA((2,)),
            pltpu.SemaphoreType.DMA((2,)),
            pltpu.SemaphoreType.DMA((2,)),
            pltpu.SemaphoreType.DMA((2,)),
        ],
        compiler_params=pltpu.CompilerParams(collective_id=0, has_side_effects=True),
        name="relayout",
    )(coords, smooth, masses, owners, meta)


def pair_kernel(fields_ref, live_ref, lists_ref, density_ref, accel_ref,
                partner8, own8, partner_t, weight_hi, weight_lo, raw, force8, force_f, sums8):
    n_ext, rows = live_ref.shape
    n_mid = n_ext - 2 * HALO
    n_own = n_mid - 2 * HALO
    live = live_ref[...] > 0
    x, y, z, h, m = (fields_ref[f] for f in range(FIELDS))
    norm_sq = x * x + y * y + z * z
    zero = jnp.zeros_like(x)
    one = jnp.ones_like(x)
    mass_log2 = jnp.where(live, jnp.log2(m), DEAD_LOG2)
    scale = LOG2E / (h * h)
    own_const = NORM_LOG2 - 3.0 * jnp.log2(h) - scale * norm_sq
    for k, v in enumerate((x, y, z, norm_sq, one, mass_log2, zero, zero)):
        partner8[pl.ds(k, n_ext, stride=8), :] = v
    twice = 2.0 * scale
    for k, v in enumerate((twice * x, twice * y, twice * z, -scale, own_const, one, zero, zero)):
        own8[pl.ds(k, n_ext, stride=8), :] = v

    def partner_step(e, carry):
        hi, mid, lo = split3(partner8[pl.ds(pl.multiple_of(e * 8, 8), 8), :])
        stack = jnp.concatenate([hi, mid, hi, mid, lo, hi], axis=0)
        partner_t[e] = stack.T.astype(BF16)
        return carry

    lax.fori_loop(0, n_ext, partner_step, 0, unroll=4)

    def weights_of(t):
        hi, mid, lo = split3(own8[pl.ds(pl.multiple_of((t + HALO) * 8, 8), 8), :])
        own = jnp.concatenate([hi, hi, mid, mid, hi, lo], axis=0).astype(BF16)
        return [jnp.exp2(jnp.dot(partner_t[lists_ref[4 * t + nb]], own, preferred_element_type=F32))
                for nb in range(4)]

    def add_up(weights):
        return sum(jnp.sum(w.reshape(rows // 8, 8, rows), axis=0) for w in weights)

    def rim_step(i, carry):
        t = jnp.where(i < HALO, i, i + n_own)
        raw[pl.ds(t, 1), :] = jnp.sum(add_up(weights_of(t)), axis=0, keepdims=True)
        return carry

    lax.fori_loop(0, 2 * HALO, rim_step, 0)

    def own_step(i, carry):
        t = i + HALO
        weights = weights_of(t)
        raw[pl.ds(t, 1), :] = jnp.sum(add_up(weights), axis=0, keepdims=True)
        for nb, w in enumerate(weights):
            hi = w.astype(BF16)
            weight_hi[i, nb * rows : (nb + 1) * rows, :] = hi
            weight_lo[i, nb * rows : (nb + 1) * rows, :] = (w - hi.astype(F32)).astype(BF16)
        return carry

    lax.fori_loop(0, n_own, own_step, 0)

    live_mid = live_ref[HALO : HALO + n_mid, :] > 0
    total = jnp.where(live_mid, raw[...], 1.0)
    q = jnp.where(live_mid, jnp.exp2(jnp.log2(total) * (-1.0 / 3.0)), 0.0)
    xm, ym, zm = (fields_ref[f, HALO : HALO + n_mid, :] for f in range(3))
    for k, v in enumerate((jnp.ones_like(q), xm, ym, zm, q, q * xm, q * ym, q * zm)):
        force8[pl.ds(k, n_mid, stride=8), :] = v

    def force_features(e, carry):
        v = force8[pl.ds(pl.multiple_of(e * 8, 8), 8), :]
        hi = v.astype(BF16)
        force_f[e] = jnp.concatenate([hi.astype(F32), v - hi.astype(F32)], axis=0).astype(BF16)
        return carry

    lax.fori_loop(0, n_mid, force_features, 0, unroll=4)

    def force_step(i, carry):
        base = 4 * (i + HALO)
        feats = jnp.concatenate([force_f[lists_ref[base + nb] - HALO] for nb in range(4)], axis=1)
        got = (jnp.dot(feats, weight_hi[i], preferred_element_type=F32)
               + jnp.dot(feats, weight_lo[i], preferred_element_type=F32))
        sums8[pl.ds(pl.multiple_of(i * 8, 8), 8), :] = got[:8] + got[8:]
        return carry

    lax.fori_loop(0, n_own, force_step, 0, unroll=2)

    mine = slice(2 * HALO, 2 * HALO + n_own)
    live_own = live_ref[mine, :] > 0
    qo = q[HALO : HALO + n_own]
    ho = fields_ref[3, mine, :]
    density_ref[...] = jnp.where(live_own, raw[HALO : HALO + n_own, :], 0.0)
    plain, pressed = (sums8[pl.ds(k, n_own, stride=8), :] for k in (0, 4))
    both = qo * plain + pressed
    factor = jnp.where(live_own, 2.0 / (ho * ho), 0.0)
    for k in range(3):
        near, far = (sums8[pl.ds(j + k, n_own, stride=8), :] for j in (1, 5))
        accel_ref[k] = factor * (fields_ref[k, mine, :] * both - (qo * near + far))


def pairs(fields, live, lists):
    n_ext, rows = live.shape
    n_mid, n_own = n_ext - 2 * HALO, n_ext - 4 * HALO
    vmem = pl.BlockSpec(memory_space=pltpu.VMEM)
    return pl.pallas_call(
        pair_kernel,
        out_shape=(jax.ShapeDtypeStruct((n_own, rows), F32), jax.ShapeDtypeStruct((3, n_own, rows), F32)),
        in_specs=[vmem, vmem, pl.BlockSpec(memory_space=pltpu.SMEM)],
        out_specs=(vmem, vmem),
        scratch_shapes=[
            pltpu.VMEM((n_ext * 8, rows), F32),
            pltpu.VMEM((n_ext * 8, rows), F32),
            pltpu.VMEM((n_ext, rows, 48), BF16),
            pltpu.VMEM((n_own, 4 * rows, rows), BF16),
            pltpu.VMEM((n_own, 4 * rows, rows), BF16),
            pltpu.VMEM((n_mid, rows), F32),
            pltpu.VMEM((n_mid * 8, rows), F32),
            pltpu.VMEM((n_mid, 16, rows), BF16),
            pltpu.VMEM((n_own * 8, rows), F32),
        ],
        name="pairs",
    )(fields, live, lists)


def per_device(coords, smooth, masses, owners, counts, neighbours):
    tile_dev, rows = smooth.shape
    flat = jnp.concatenate([counts, neighbours.reshape(-1)])
    pad = -flat.shape[0] % 128
    meta = jnp.pad(flat, (0, pad)).reshape(-1, 128)
    fields, rims = relayout(coords, smooth, masses, owners.reshape(1, -1), meta)
    rims = rims.reshape(2, -1)
    rim_counts, rim_lists = rims[:, :tile_dev], rims[:, tile_dev : 5 * tile_dev].reshape(2, tile_dev, 4)
    all_counts = jnp.concatenate([rim_counts[0, -2 * HALO :], counts, rim_counts[1, : 2 * HALO]])
    live = (jnp.arange(rows, dtype=jnp.int32)[None, :] < all_counts[:, None]).astype(jnp.int32)
    lists = jnp.concatenate([
        rim_lists[0, -HALO:] + (HALO - tile_dev), neighbours + HALO, rim_lists[1, :HALO] + (HALO + tile_dev),
    ]).reshape(-1)
    return pairs(fields, live, lists)


def solution(mesh):
    rs = ("region", "sub")
    in_specs = (P(None, rs, None), P(rs, None), P(rs, None), P(rs), P(rs), P(rs, None))
    out_specs = (P(rs, None), P(None, rs, None))
    return jax.shard_map(per_device, mesh=mesh, in_specs=in_specs, out_specs=out_specs, check_vma=False)
```

time: 120 us -> 60.5 us (0.50)
  other arithmetic: 66 us -> 1.69 us
  Pallas kernels: 0 us -> 54.7 us
  starting transfers between devices: 32.2 us -> 0 us
  waiting for transfers between devices: 16.6 us -> 0 us
    pallas_call x0 -> x2, Pallas kernels: none -> 54.7 us  [the longest x1 30.2 us: relayout(): pl.pallas_call(functools.partial(relayout_kernel, regions, subs), out_sha...]
    reduce_sum x3 -> x0, other arithmetic: 48.8 us -> none  [the longest x1 20.6 us: force_pass(): accel_sum = accel_sum + jnp.sum(offset_vec * coefficient[None], axis=-1)]
    ppermute x4 -> x0, starting transfers between devices: 18.4 us -> none  [the longest x2 13.2 us: extended_2(): after = lax.ppermute(initial, axis, down)]
    all_to_all x1 -> x0, starting transfers between devices: 13.8 us -> none  [per_device(): lax.all_to_all(grouped, 'region', split_axis=1, concat_axis=1, tiled=True)]
    mul x5 -> x0, other arithmetic: 10 us -> none  [the longest x1 7.85 us: force_pass(): weight_pair * partner[4][:, None, :]]
    ppermute x4 -> x0, waiting for transfers between devices: 9.38 us -> none  [the longest x2 9.38 us: extended_2(): before = lax.ppermute(last, axis, up)]
    all_to_all x1 -> x0, waiting for transfers between devices: 7.19 us -> none  [per_device(): lax.all_to_all(grouped, 'region', split_axis=1, concat_axis=1, tiled=True)]
    sort x1 -> x0, other arithmetic: 2.69 us -> none  [per_device(): ordering = jnp.argsort(owners, stable=True)]
  transfers between devices with their start and end apart: 5 -> 0, of which waited for: 3 -> 0; matrix products, arithmetic and copies ran while one was open for 3% -> 0% of each run, Pallas kernels for 0% -> 0%
where the time goes in v1:
time: 60.5 us; the launch traced here: 60.3 us
  Pallas kernels  54.7 us (90%)
  local copies, waits for them, and re-layouts  3.21 us (5%)
  other arithmetic  1.69 us (3%)
  between operations  0.68 us (1%)
    pallas_call x1, Pallas kernels, relayout(): pl.pallas_call(functools.partial(relayout_kernel, regions, subs), out_sha...  30.2 us
    pallas_call x1, Pallas kernels, pairs(): pl.pallas_call(pair_kernel, out_shape=(jax.ShapeDtypeStruct((n_own, rows)...  24.5 us
    unnamed x8, local copies, waits for them, and re-layouts  1.32 us

profile of v1, /device:TPU:1, one launch (start us, length us, event | category | flops | bytes accessed | tf_op | source)
XLA Modules:
  0.0 60.3 jit_solution(14883998099605625742)
XLA Ops:
  0.6 0.0 copy-start
  0.6 0.7 %broadcast_add_fusion = s32[64,4]{0,1:T(4,128)S(1)} fusion(s32[64,4]{0,1:T(4,128)} %param.11), kind=kLoop, calls=%fused_computation.10 | loop fusion | flops 256 | bytes 2048 | tf_op jit(solution)/shard_map/add | solution.py:278
  1.4 0.0 copy-done
  1.4 0.1 copy.10
  1.5 0.0 copy-start.2
  1.5 0.1 reshape.28
  1.6 0.5 copy-done.2
  2.1 0.1 pad_add_fusion
  2.2 0.6 pad_bitcast_fusion.meta_ref
  2.8 30.2 %relayout.1 = (f32[5,80,128]{2,1,0:T(8,128)}, s32[2,3,128]{2,1,0:T(4,128)}) custom-call(f32[3,64,128]{2,1,0:T(8,128)} %coords_ref.1, f32[64,128]{1,0:T(8,128)} %smooth_ref.1, f32[64,128]{1,0:T(8,128)} %masses_ref.1, s32[1,64]{1,0:T(1,128)} %bitcast.18, s32[3,128]{1,0:T(4,128)} %pad_bitcast_fusion.meta_ref), custom_call_target="tpu_custom_call" | custom-call | tf_op jit(solution)/shard_map/relayout/pallas_call | solution.py:128
  33.0 0.0 copy-start.1
  33.0 0.7 %copy-done.1 = s32[2,3,128]{2,1,0:T(4,128)S(1)} copy-done((s32[2,3,128]{2,1,0:T(4,128)S(1)}, s32[2,3,128]{2,1,0:T(4,128)}, u32[]{:S(2)}) %copy-start.1) | copy-done | bytes 3096
  33.7 0.1 slice_bitcast_fusion.1
  33.8 0.1 slice.25
  33.8 0.1 pad_add_fusion.2
  33.9 0.7 %fusion.live_ref = s32[80,128]{1,0:T(8,128)} fusion(s32[80]{0:T(128)S(1)} %pad_add_fusion.2), kind=kLoop, calls=%fused_computation.1 | loop fusion | flops 20480 | bytes 41280 | tf_op jit(solution)/shard_map/convert_element_type | solution.py:276
  34.6 0.1 reshape.31
  34.8 0.1 copy.11
  34.9 0.1 copy.12
  34.9 0.1 pad_add_fusion.1
  35.0 0.1 copy.13
  35.1 0.7 %reshape.32.lists_ref = s32[288]{0:T(512)} reshape(s32[72,4]{1,0:T(8,128)S(1)} %copy.13) | data formatting | bytes 2304 | tf_op jit(solution)/shard_map/reshape | solution.py:279
  35.8 24.5 %pairs.1 = (f32[64,128]{1,0:T(8,128)}, f32[3,64,128]{2,1,0:T(8,128)}) custom-call(f32[5,80,128]{2,1,0:T(8,128)} %get-tuple-element.4.fields_ref, s32[80,128]{1,0:T(8,128)} %fusion.live_ref, s32[288]{0:T(512)} %reshape.32.lists_ref), custom_call_target="tpu_custom_call" | custom-call | tf_op jit(solution)/shard_map/pairs/pallas_call | solution.py:247
  (2 shorter events, 0.0 us)
Async XLA Ops:
  0.6 0.8 %copy-start = (s32[64,4]{0,1:T(4,128)S(1)}, s32[64,4]{0,1:T(4,128)}, u32[]{:S(2)}) copy-start(s32[64,4]{0,1:T(4,128)} %param.11) | copy-start | bytes 3076
  1.5 0.7 %copy-start.2 = (s32[64]{0:T(128)S(1)}, s32[64]{0:T(128)}, u32[]{:S(2)}) copy-start(s32[64]{0:T(128)} %param.10) | copy-start | bytes 772
  33.0 0.7 %copy-start.1 = (s32[2,3,128]{2,1,0:T(4,128)S(1)}, s32[2,3,128]{2,1,0:T(4,128)}, u32[]{:S(2)}) copy-start(s32[2,3,128]{2,1,0:T(4,128)} %get-tuple-element.5) | copy-start | bytes 9220

commit v2 on v1

v2 whole, which is shorter than its diff:
```python
import functools
import math

import jax
import jax.numpy as jnp
from jax import lax
from jax.experimental import pallas as pl
from jax.experimental.pallas import tpu as pltpu
from jax.sharding import PartitionSpec as P

HALO = 4
RIM = 2 * HALO
FIELDS = 5
UNROLL = 8
LOG2E = math.log2(math.e)
NORM_LOG2 = -1.5 * math.log2(math.pi)
DEAD_LOG2 = -1000.0
MESH = pl.DeviceIdType.MESH
F32 = jnp.float32
BF16 = jnp.bfloat16


def split3(v):
    hi = v.astype(BF16).astype(F32)
    rest = v - hi
    mid = rest.astype(BF16).astype(F32)
    return hi, mid, rest - mid


def kernel(regions, subs, coords_hbm, smooth_hbm, masses_hbm, owners_hbm, counts_hbm, lists_hbm,
           density_ref, accel_ref,
           coords, smooth, masses, owners, counts, lists, rim_counts_v, rim_lists_v, rim_counts, rim_lists,
           packed, landed, fields, live, partner8, own8, partner_t, weight_hi, weight_lo, raw, force8, force_f, sums8,
           in_sem, send_sem, recv_sem, rim_send, rim_recv, meta_send, meta_recv, meta_sem):
    tile_dev, rows = smooth.shape
    group = tile_dev // regions
    rim = RIM // group
    r = lax.axis_index("region")
    s = lax.axis_index("sub")
    up = lax.rem(s + 1, subs)
    down = lax.rem(s + subs - 1, subs)

    barrier = pltpu.get_barrier_semaphore()
    for off in range(1, regions):
        pl.semaphore_signal(barrier, inc=1, device_id=(lax.rem(r + off, regions), s), device_id_type=MESH)
    for peer in (up, down):
        pl.semaphore_signal(barrier, inc=1, device_id=(r, peer), device_id_type=MESH)
    loads = [pltpu.make_async_copy(src, dst, in_sem.at[n]) for n, (src, dst) in enumerate((
        (owners_hbm, owners), (coords_hbm, coords), (smooth_hbm, smooth), (masses_hbm, masses),
        (counts_hbm, counts), (lists_hbm, lists)))]
    for load in loads:
        load.start()

    loads[0].wait()
    own = owners[...]
    hot = (lax.broadcasted_iota(jnp.int32, (regions, tile_dev), 0) == own).astype(F32)
    before = (lax.broadcasted_iota(jnp.int32, (tile_dev, tile_dev), 0)
              < lax.broadcasted_iota(jnp.int32, (tile_dev, tile_dev), 1)).astype(F32)
    count = jnp.dot(hot.astype(BF16), before.astype(BF16), preferred_element_type=F32)
    rank = jnp.sum(hot * count, axis=0, keepdims=True).astype(jnp.int32)
    place = own * 8 + rank
    pick = (lax.broadcasted_iota(jnp.int32, (8 * regions, tile_dev), 0) == place).astype(F32)
    pick3 = jnp.concatenate([pick, pick, pick], axis=1).astype(BF16)
    for load in loads[1:4]:
        load.wait()
    for f in range(FIELDS):
        field = coords[f] if f < 3 else (smooth[...] if f == 3 else masses[...])
        stack = jnp.concatenate(split3(field), axis=0).astype(BF16)
        got = jnp.dot(pick3, stack, preferred_element_type=F32)
        for d in range(regions):
            packed[d, pl.ds(f, group, stride=FIELDS), :] = got[8 * d : 8 * d + group]

    pl.semaphore_wait(barrier, regions - 1 + 2)

    offsets = sorted(range(1, regions), key=lambda o: -min(o, regions - o))
    copies = []
    for off in offsets:
        dst = lax.rem(r + off, regions)
        copies.append(pltpu.make_async_remote_copy(
            src_ref=packed.at[dst], dst_ref=landed.at[rim + r], send_sem=send_sem.at[off],
            recv_sem=recv_sem.at[r], device_id=(dst, s), device_id_type=MESH))
    metas = [
        pltpu.make_async_remote_copy(
            src_ref=src, dst_ref=dst.at[slot], send_sem=meta_send.at[2 * n + slot],
            recv_sem=meta_recv.at[2 * n + slot], device_id=(r, peer), device_id_type=MESH)
        for slot, peer in enumerate((up, down))
        for n, (src, dst) in enumerate(((counts_hbm, rim_counts_v), (lists_hbm, rim_lists_v)))]
    for copy in copies + metas:
        copy.start()
    landed[rim + r] = packed[r]

    def arrived(src):
        @pl.when(src != r)
        def _():
            pltpu.make_async_remote_copy(
                src_ref=packed.at[src], dst_ref=landed.at[rim + src], send_sem=send_sem.at[0],
                recv_sem=recv_sem.at[src], device_id=(src, s), device_id_type=MESH).wait_recv()

    first = list(range(rim))
    first += [g for g in range(regions - rim, regions) if g not in first]
    for src in first:
        arrived(src)
    rims = [
        pltpu.make_async_remote_copy(
            src_ref=landed.at[pl.ds(rim, rim)], dst_ref=landed.at[pl.ds(rim + regions, rim)],
            send_sem=rim_send.at[0], recv_sem=rim_recv.at[0], device_id=(r, down), device_id_type=MESH),
        pltpu.make_async_remote_copy(
            src_ref=landed.at[pl.ds(regions, rim)], dst_ref=landed.at[pl.ds(0, rim)],
            send_sem=rim_send.at[1], recv_sem=rim_recv.at[1], device_id=(r, up), device_id_type=MESH),
    ]
    for copy in rims:
        copy.start()

    lane = lax.broadcasted_iota(jnp.int32, (1, rows), 1)
    for load in loads[4:]:
        load.wait()

    def live_step(t, carry):
        live[pl.ds(t + RIM, 1), :] = (lane < counts[0, t]).astype(F32)
        return carry

    lax.fori_loop(0, tile_dev, live_step, 0, unroll=UNROLL)
    for src in range(regions):
        if src not in first:
            arrived(src)

    def unpack(groups):
        for g in groups:
            for f in range(FIELDS):
                fields[f, group * g : group * (g + 1), :] = landed[g, pl.ds(f, group, stride=FIELDS), :]

    def pair_features(a, b):
        x, y, z, h, m = (fields[f, a:b, :] for f in range(FIELDS))
        norm_sq = x * x + y * y + z * z
        zero, one = jnp.zeros_like(x), jnp.ones_like(x)
        mass_log2 = jnp.where(live[a:b, :] > 0, jnp.log2(m), DEAD_LOG2)
        scale = LOG2E / (h * h)
        own_const = NORM_LOG2 - 3.0 * jnp.log2(h) - scale * norm_sq
        twice = 2.0 * scale
        for k, v in enumerate((x, y, z, norm_sq, one, mass_log2, zero, zero)):
            partner8[pl.ds(8 * a + k, b - a, stride=8), :] = v
        for k, v in enumerate((twice * x, twice * y, twice * z, -scale, own_const, one, zero, zero)):
            own8[pl.ds(8 * a + k, b - a, stride=8), :] = v

        def partner_step(e, carry):
            hi, mid, lo = split3(partner8[pl.ds(pl.multiple_of(e * 8, 8), 8), :])
            partner_t[e] = jnp.concatenate([hi, mid, hi, mid, lo, hi], axis=0).T.astype(BF16)
            return carry

        lax.fori_loop(a, b, partner_step, 0, unroll=UNROLL)

    def density_of(e, partners, slot):
        hi, mid, lo = split3(own8[pl.ds(pl.multiple_of(e * 8, 8), 8), :])
        mine = jnp.concatenate([hi, hi, mid, mid, hi, lo], axis=0).astype(BF16)
        total = None
        for nb, partner in enumerate(partners):
            w = jnp.exp2(jnp.dot(partner_t[partner], mine, preferred_element_type=F32))
            part = jnp.sum(w.reshape(rows // 8, 8, rows), axis=0)
            total = part if total is None else total + part
            if slot is not None:
                high = w.astype(BF16)
                weight_hi[slot, nb * rows : (nb + 1) * rows, :] = high
                weight_lo[slot, nb * rows : (nb + 1) * rows, :] = (w - high.astype(F32)).astype(BF16)
        raw[pl.ds(e, 1), :] = jnp.sum(total, axis=0, keepdims=True)

    def own_partners(t):
        return [lists[nb, t] + HALO for nb in range(4)]

    def pressures(a, b):
        alive = live[a:b, :] > 0
        total = jnp.where(alive, raw[a:b, :], 1.0)
        return jnp.where(alive, jnp.exp2(jnp.log2(total) * (-1.0 / 3.0)), 0.0)

    def force_features(a, b):
        q = pressures(a, b)
        x, y, z = (fields[f, a:b, :] for f in range(3))
        for k, v in enumerate((jnp.ones_like(q), x, y, z, q, q * x, q * y, q * z)):
            force8[pl.ds(8 * a + k, b - a, stride=8), :] = v

        def step(e, carry):
            v = force8[pl.ds(pl.multiple_of(e * 8, 8), 8), :]
            hi = v.astype(BF16).astype(F32)
            force_f[e] = jnp.concatenate([hi, v - hi], axis=0).astype(BF16)
            return carry

        lax.fori_loop(a, b, step, 0, unroll=UNROLL)

    def force_of(t):
        feats = jnp.concatenate([force_f[p] for p in own_partners(t)], axis=1)
        got = (jnp.dot(feats, weight_hi[t], preferred_element_type=F32)
               + jnp.dot(feats, weight_lo[t], preferred_element_type=F32))
        sums8[pl.ds(pl.multiple_of(t * 8, 8), 8), :] = got[:8] + got[8:]

    def finish(a, b):
        alive = live[RIM + a : RIM + b, :] > 0
        q = pressures(RIM + a, RIM + b)
        h = fields[3, RIM + a : RIM + b, :]
        density_ref[a:b, :] = jnp.where(alive, raw[RIM + a : RIM + b, :], 0.0)
        plain, pressed = (sums8[pl.ds(8 * a + k, b - a, stride=8), :] for k in (0, 4))
        both = q * plain + pressed
        factor = jnp.where(alive, 2.0 / (h * h), 0.0)
        for k in range(3):
            near, far = (sums8[pl.ds(8 * a + j + k, b - a, stride=8), :] for j in (1, 5))
            accel_ref[k, a:b, :] = factor * (fields[k, RIM + a : RIM + b, :] * both - (q * near + far))

    def inner_density(t, carry):
        density_of(t + RIM, own_partners(t), t)
        return carry

    def inner_force(t, carry):
        force_of(t)
        return carry

    top = RIM + tile_dev
    unpack(range(rim, rim + regions))
    pair_features(RIM, top)
    lax.fori_loop(HALO, tile_dev - HALO, inner_density, 0, unroll=UNROLL)
    force_features(RIM, top)
    lax.fori_loop(RIM, tile_dev - RIM, inner_force, 0, unroll=UNROLL)
    finish(RIM, tile_dev - RIM)

    for copy in metas:
        copy.wait_recv()
    moves = [pltpu.make_async_copy(rim_counts_v, rim_counts, meta_sem.at[0]),
             pltpu.make_async_copy(rim_lists_v, rim_lists, meta_sem.at[1])]
    for move in moves:
        move.start()
    for move in moves:
        move.wait()
    for copy in rims:
        copy.wait_recv()
    for k in range(RIM):
        live[k : k + 1, :] = (lane < rim_counts[0, 0, tile_dev - RIM + k]).astype(F32)
        live[top + k : top + k + 1, :] = (lane < rim_counts[1, 0, k]).astype(F32)
    unpack(list(range(rim)) + list(range(rim + regions, 2 * rim + regions)))
    pair_features(0, RIM)
    pair_features(top, top + RIM)
    for k in range(HALO):
        below = [jnp.maximum(rim_lists[0, nb, tile_dev - HALO + k] + (HALO - tile_dev), 0) for nb in range(4)]
        density_of(HALO + k, below, None)
        density_of(RIM + k, own_partners(k), k)
        density_of(top - HALO + k, own_partners(tile_dev - HALO + k), tile_dev - HALO + k)
        above = [rim_lists[1, nb, k] + (HALO + tile_dev) for nb in range(4)]
        density_of(top + k, above, None)
    force_features(0, 2 * RIM)
    force_features(top - RIM, top + RIM)
    for k in range(RIM):
        force_of(k)
        force_of(tile_dev - RIM + k)
    finish(0, RIM)
    finish(tile_dev - RIM, tile_dev)
    for copy in copies + metas + rims:
        copy.wait_send()


def per_device(coords, smooth, masses, owners, counts, neighbours):
    regions, subs = lax.axis_size("region"), lax.axis_size("sub")
    tile_dev, rows = smooth.shape
    group = tile_dev // regions
    groups = regions + 2 * (RIM // group)
    ext = tile_dev + 2 * RIM
    owners, counts, lists = owners.reshape(1, -1), counts.reshape(1, -1), neighbours.T
    vmem = pl.BlockSpec(memory_space=pltpu.VMEM)
    dma = pltpu.SemaphoreType.DMA
    return pl.pallas_call(
        functools.partial(kernel, regions, subs),
        out_shape=(jax.ShapeDtypeStruct((tile_dev, rows), F32), jax.ShapeDtypeStruct((3, tile_dev, rows), F32)),
        in_specs=[pl.BlockSpec(memory_space=pl.ANY)] * 6,
        out_specs=(vmem, vmem),
        scratch_shapes=[
            pltpu.VMEM(coords.shape, F32), pltpu.VMEM(smooth.shape, F32), pltpu.VMEM(masses.shape, F32),
            pltpu.VMEM(owners.shape, jnp.int32),
            pltpu.SMEM(counts.shape, jnp.int32), pltpu.SMEM(lists.shape, jnp.int32),
            pltpu.VMEM((2,) + counts.shape, jnp.int32), pltpu.VMEM((2,) + lists.shape, jnp.int32),
            pltpu.SMEM((2,) + counts.shape, jnp.int32), pltpu.SMEM((2,) + lists.shape, jnp.int32),
            pltpu.VMEM((regions, group * FIELDS, rows), F32),
            pltpu.VMEM((groups, group * FIELDS, rows), F32),
            pltpu.VMEM((FIELDS, ext, rows), F32),
            pltpu.VMEM((ext, rows), F32),
            pltpu.VMEM((ext * 8, rows), F32),
            pltpu.VMEM((ext * 8, rows), F32),
            pltpu.VMEM((ext, rows, 48), BF16),
            pltpu.VMEM((tile_dev, 4 * rows, rows), BF16),
            pltpu.VMEM((tile_dev, 4 * rows, rows), BF16),
            pltpu.VMEM((ext, rows), F32),
            pltpu.VMEM((ext * 8, rows), F32),
            pltpu.VMEM((ext, 16, rows), BF16),
            pltpu.VMEM((tile_dev * 8, rows), F32),
            dma((6,)), dma((regions,)), dma((regions,)), dma((2,)), dma((2,)), dma((4,)), dma((4,)), dma((2,)),
        ],
        compiler_params=pltpu.CompilerParams(collective_id=0, has_side_effects=True),
        name="sph",
    )(coords, smooth, masses, owners, counts, lists)


def solution(mesh):
    rs = ("region", "sub")
    in_specs = (P(None, rs, None), P(rs, None), P(rs, None), P(rs), P(rs), P(rs, None))
    out_specs = (P(rs, None), P(None, rs, None))
    return jax.shard_map(per_device, mesh=mesh, in_specs=in_specs, out_specs=out_specs, check_vma=False)
```

time: 60.5 us -> 41.2 us (0.68)
  Pallas kernels: 54.7 us -> 37.4 us
  other arithmetic: 1.69 us -> 0 us
    pallas_call x2 -> x1, Pallas kernels: 54.7 us -> 37.4 us  [per_device(): pl.pallas_call(functools.partial(kernel, regions, subs), out_shape=(jax.S...]
    unnamed x8 -> x2, local copies, waits for them, and re-layouts: 1.32 us -> 2.91 us
    reshape x4 -> x0, local copies, waits for them, and re-layouts: 1.46 us -> none  [the longest x1 0.67 us: per_device(): lists = jnp.concatenate([rim_lists[0, -HALO:] + (HALO - tile_dev), neighb...]
    add x2 -> x0, other arithmetic: 0.75 us -> none  [the longest x1 0.75 us: per_device(): neighbours + HALO]
    convert_element_type x1 -> x0, other arithmetic: 0.71 us -> none  [per_device(): (jnp.arange(rows, dtype=jnp.int32)[None, :] < all_counts[:, None]).astype...]
where the time goes in v2:
time: 41.2 us; the launch traced here: 41 us
  Pallas kernels  37.4 us (91%)
  local copies, waits for them, and re-layouts  2.91 us (7%)
  between operations  0.64 us (2%)
    pallas_call x1, Pallas kernels, per_device(): pl.pallas_call(functools.partial(kernel, regions, subs), out_shape=(jax.S...  37.4 us
    unnamed x2, local copies, waits for them, and re-layouts  2.91 us

profile of v2, /device:TPU:1, one launch (start us, length us, event | category | flops | bytes accessed | tf_op | source)
XLA Modules:
  0.0 41.0 jit_solution(4650067846000339899)
XLA Ops:
  0.6 37.4 %sph.1 = (f32[64,128]{1,0:T(8,128)}, f32[3,64,128]{2,1,0:T(8,128)}) custom-call(f32[3,64,128]{2,1,0:T(8,128)} %coords_hbm.1, f32[64,128]{1,0:T(8,128)} %smooth_hbm.1, f32[64,128]{1,0:T(8,128)} %masses_hbm.1, s32[1,64]{1,0:T(1,128)} %bitcast.4, s32[1,64]{1,0:T(1,128)} %bitcast.5, s32[4,64]{1,0:T(4,128)} %bitcast.3), custom_call_target="tpu_custom_call" | custom-call | tf_op jit(solution)/shard_map/sph/pallas_call | solution.py:265
  38.0 1.4 %copy.10 = f32[64,128]{1,0:T(8,128)} copy(f32[64,128]{1,0:T(8,128)} %get-tuple-element.4) | data formatting | bytes 65536
  39.4 1.5 %copy.11 = f32[3,64,128]{2,1,0:T(8,128)} copy(f32[3,64,128]{2,1,0:T(8,128)} %get-tuple-element.5) | data formatting | bytes 196608

commit v3 on v2

--- a/solution.py
+++ b/solution.py
@@ -12,6 +12,7 @@
 RIM = 2 * HALO
 FIELDS = 5
 UNROLL = 8
+SUB_RUN = 12
 LOG2E = math.log2(math.e)
 NORM_LOG2 = -1.5 * math.log2(math.pi)
 DEAD_LOG2 = -1000.0
@@ -31,7 +32,7 @@
            density_ref, accel_ref,
            coords, smooth, masses, owners, counts, lists, rim_counts_v, rim_lists_v, rim_counts, rim_lists,
            packed, landed, fields, live, partner8, own8, partner_t, weight_hi, weight_lo, raw, force8, force_f, sums8,
-           in_sem, send_sem, recv_sem, rim_send, rim_recv, meta_send, meta_recv, meta_sem):
+           in_sem, send_sem, recv_sem, rim_send, rim_recv, meta_send, meta_recv, meta_sem, ok, rim_ok):
     tile_dev, rows = smooth.shape
     group = tile_dev // regions
     rim = RIM // group
@@ -40,16 +41,57 @@
     up = lax.rem(s + 1, subs)
     down = lax.rem(s + subs - 1, subs)
 
+    run = lax.rem(s, SUB_RUN) if subs % SUB_RUN == 0 else s
+    last_run = (SUB_RUN if subs % SUB_RUN == 0 else subs) - 1
+    down_earlier = run > 0
+    up_earlier = run == last_run
+
+    def order(i):
+        chips = regions // 2
+        y = i // 2
+        place = 2 * jnp.where(y < chips // 2, y, chips + chips // 2 - 1 - y) + lax.rem(i, 2)
+        return jnp.where(s == 0, jnp.where(i == 0, regions - 1, place - 1), place)
+
+    mine = order(r)
+    peers = [lax.rem(r + off, regions) for off in sorted(range(1, regions), key=lambda o: -min(o, regions - o))]
+    later = [order(p) > mine for p in peers]
+
+    def when_each(conditions, action):
+        for n, condition in enumerate(conditions):
+            pl.when(condition)(functools.partial(action, n))
+
     barrier = pltpu.get_barrier_semaphore()
-    for off in range(1, regions):
-        pl.semaphore_signal(barrier, inc=1, device_id=(lax.rem(r + off, regions), s), device_id_type=MESH)
-    for peer in (up, down):
-        pl.semaphore_signal(barrier, inc=1, device_id=(r, peer), device_id_type=MESH)
+
+    def greet(n):
+        pl.semaphore_signal(barrier, inc=1, device_id=(peers[n], s), device_id_type=MESH)
+
+    when_each(later, greet)
+
+    def greet_rim(n):
+        pl.semaphore_signal(barrier, inc=1, device_id=(r, (up, down)[n]), device_id_type=MESH)
+
+    when_each([jnp.logical_not(up_earlier), jnp.logical_not(down_earlier)], greet_rim)
     loads = [pltpu.make_async_copy(src, dst, in_sem.at[n]) for n, (src, dst) in enumerate((
         (owners_hbm, owners), (coords_hbm, coords), (smooth_hbm, smooth), (masses_hbm, masses),
         (counts_hbm, counts), (lists_hbm, lists)))]
     for load in loads:
         load.start()
+    expected = mine + down_earlier.astype(jnp.int32) + up_earlier.astype(jnp.int32)
+
+    @pl.when(expected > 0)
+    def _():
+        pl.semaphore_wait(barrier, expected)
+
+    def answer(n):
+        pl.semaphore_signal(ok, inc=1, device_id=(peers[n], s), device_id_type=MESH)
+
+    earlier = [jnp.logical_not(c) for c in later]
+    when_each(earlier, answer)
+
+    def answer_rim(n):
+        pl.semaphore_signal(rim_ok.at[1 - n], inc=1, device_id=(r, (up, down)[n]), device_id_type=MESH)
+
+    when_each([up_earlier, down_earlier], answer_rim)
 
     loads[0].wait()
     own = owners[...]
@@ -70,23 +112,38 @@
         for d in range(regions):
             packed[d, pl.ds(f, group, stride=FIELDS), :] = got[8 * d : 8 * d + group]
 
-    pl.semaphore_wait(barrier, regions - 1 + 2)
-
-    offsets = sorted(range(1, regions), key=lambda o: -min(o, regions - o))
-    copies = []
-    for off in offsets:
-        dst = lax.rem(r + off, regions)
-        copies.append(pltpu.make_async_remote_copy(
-            src_ref=packed.at[dst], dst_ref=landed.at[rim + r], send_sem=send_sem.at[off],
-            recv_sem=recv_sem.at[r], device_id=(dst, s), device_id_type=MESH))
-    metas = [
+    copies = [pltpu.make_async_remote_copy(
+        src_ref=packed.at[dst], dst_ref=landed.at[rim + r], send_sem=send_sem.at[n],
+        recv_sem=recv_sem.at[r], device_id=(dst, s), device_id_type=MESH) for n, dst in enumerate(peers)]
+    metas = [[
         pltpu.make_async_remote_copy(
             src_ref=src, dst_ref=dst.at[slot], send_sem=meta_send.at[2 * n + slot],
             recv_sem=meta_recv.at[2 * n + slot], device_id=(r, peer), device_id_type=MESH)
-        for slot, peer in enumerate((up, down))
         for n, (src, dst) in enumerate(((counts_hbm, rim_counts_v), (lists_hbm, rim_lists_v)))]
-    for copy in copies + metas:
-        copy.start()
+        for slot, peer in enumerate((up, down))]
+    rims = [
+        pltpu.make_async_remote_copy(
+            src_ref=landed.at[pl.ds(regions, rim)], dst_ref=landed.at[pl.ds(0, rim)],
+            send_sem=rim_send.at[0], recv_sem=rim_recv.at[0], device_id=(r, up), device_id_type=MESH),
+        pltpu.make_async_remote_copy(
+            src_ref=landed.at[pl.ds(rim, rim)], dst_ref=landed.at[pl.ds(rim + regions, rim)],
+            send_sem=rim_send.at[1], recv_sem=rim_recv.at[1], device_id=(r, down), device_id_type=MESH),
+    ]
+
+    def send_meta(slot):
+        for copy in metas[slot]:
+            copy.start()
+
+    def send_rim(slot):
+        rims[slot].start()
+
+    def answered_rim(slot):
+        pl.semaphore_wait(rim_ok.at[slot], 1)
+        send_meta(slot)
+        send_rim(slot)
+
+    when_each(earlier, lambda n: copies[n].start())
+    when_each([up_earlier, down_earlier], send_meta)
     landed[rim + r] = packed[r]
 
     def arrived(src):
@@ -96,20 +153,17 @@
                 src_ref=packed.at[src], dst_ref=landed.at[rim + src], send_sem=send_sem.at[0],
                 recv_sem=recv_sem.at[src], device_id=(src, s), device_id_type=MESH).wait_recv()
 
+    @pl.when(mine < regions - 1)
+    def _():
+        pl.semaphore_wait(ok, regions - 1 - mine)
+
+    when_each(later, lambda n: copies[n].start())
     first = list(range(rim))
     first += [g for g in range(regions - rim, regions) if g not in first]
     for src in first:
         arrived(src)
-    rims = [
-        pltpu.make_async_remote_copy(
-            src_ref=landed.at[pl.ds(rim, rim)], dst_ref=landed.at[pl.ds(rim + regions, rim)],
-            send_sem=rim_send.at[0], recv_sem=rim_recv.at[0], device_id=(r, down), device_id_type=MESH),
-        pltpu.make_async_remote_copy(
-            src_ref=landed.at[pl.ds(regions, rim)], dst_ref=landed.at[pl.ds(0, rim)],
-            send_sem=rim_send.at[1], recv_sem=rim_recv.at[1], device_id=(r, up), device_id_type=MESH),
-    ]
-    for copy in rims:
-        copy.start()
+    when_each([up_earlier, down_earlier], send_rim)
+    pl.when(jnp.logical_not(up_earlier))(functools.partial(answered_rim, 0))
 
     lane = lax.broadcasted_iota(jnp.int32, (1, rows), 1)
     for load in loads[4:]:
@@ -219,7 +273,9 @@
     lax.fori_loop(RIM, tile_dev - RIM, inner_force, 0, unroll=UNROLL)
     finish(RIM, tile_dev - RIM)
 
-    for copy in metas:
+    pl.when(jnp.logical_not(down_earlier))(functools.partial(answered_rim, 1))
+
+    for copy in metas[0] + metas[1]:
         copy.wait_recv()
     moves = [pltpu.make_async_copy(rim_counts_v, rim_counts, meta_sem.at[0]),
              pltpu.make_async_copy(rim_lists_v, rim_lists, meta_sem.at[1])]
@@ -227,29 +283,34 @@
         move.start()
     for move in moves:
         move.wait()
-    for copy in rims:
-        copy.wait_recv()
     for k in range(RIM):
         live[k : k + 1, :] = (lane < rim_counts[0, 0, tile_dev - RIM + k]).astype(F32)
         live[top + k : top + k + 1, :] = (lane < rim_counts[1, 0, k]).astype(F32)
-    unpack(list(range(rim)) + list(range(rim + regions, 2 * rim + regions)))
+
+    rims[1].wait_recv()
+    unpack(range(rim + regions, 2 * rim + regions))
+    pair_features(top, top + RIM)
+    for k in range(HALO):
+        density_of(top - HALO + k, own_partners(tile_dev - HALO + k), tile_dev - HALO + k)
+        above = [rim_lists[1, nb, k] + (HALO + tile_dev) for nb in range(4)]
+        density_of(top + k, above, None)
+    force_features(top - RIM, top + RIM)
+    for k in range(RIM):
+        force_of(tile_dev - RIM + k)
+    finish(tile_dev - RIM, tile_dev)
+
+    rims[0].wait_recv()
+    unpack(range(rim))
     pair_features(0, RIM)
-    pair_features(top, top + RIM)
     for k in range(HALO):
         below = [jnp.maximum(rim_lists[0, nb, tile_dev - HALO + k] + (HALO - tile_dev), 0) for nb in range(4)]
         density_of(HALO + k, below, None)
         density_of(RIM + k, own_partners(k), k)
-        density_of(top - HALO + k, own_partners(tile_dev - HALO + k), tile_dev - HALO + k)
-        above = [rim_lists[1, nb, k] + (HALO + tile_dev) for nb in range(4)]
-        density_of(top + k, above, None)
     force_features(0, 2 * RIM)
-    force_features(top - RIM, top + RIM)
     for k in range(RIM):
         force_of(k)
-        force_of(tile_dev - RIM + k)
     finish(0, RIM)
-    finish(tile_dev - RIM, tile_dev)
-    for copy in copies + metas + rims:
+    for copy in copies + metas[0] + metas[1] + rims:
         copy.wait_send()
 
 
@@ -264,7 +325,7 @@
     dma = pltpu.SemaphoreType.DMA
     return pl.pallas_call(
         functools.partial(kernel, regions, subs),
-        out_shape=(jax.ShapeDtypeStruct((tile_dev, rows), F32), jax.ShapeDtypeStruct((3, tile_dev, rows), F32)),
+        out_shape=(pltpu.VMEM((tile_dev, rows), F32), pltpu.VMEM((3, tile_dev, rows), F32)),
         in_specs=[pl.BlockSpec(memory_space=pl.ANY)] * 6,
         out_specs=(vmem, vmem),
         scratch_shapes=[
@@ -287,6 +348,7 @@
             pltpu.VMEM((ext, 16, rows), BF16),
             pltpu.VMEM((tile_dev * 8, rows), F32),
             dma((6,)), dma((regions,)), dma((regions,)), dma((2,)), dma((2,)), dma((4,)), dma((4,)), dma((2,)),
+            pltpu.SemaphoreType.REGULAR, pltpu.SemaphoreType.REGULAR((2,)),
         ],
         compiler_params=pltpu.CompilerParams(collective_id=0, has_side_effects=True),
         name="sph",

time: 41.2 us -> 32.6 us (0.79)
  Pallas kernels: 37.4 us -> 30.4 us
  local copies, waits for them, and re-layouts: 2.91 us -> 1.26 us
    pallas_call x1, Pallas kernels: 37.4 us -> 30.4 us  [per_device(): pl.pallas_call(functools.partial(kernel, regions, subs), out_shape=(pltpu...]
    unnamed x2, local copies, waits for them, and re-layouts: 2.91 us -> 1.26 us
where the time goes in v3:
time: 32.6 us; the launch traced here: 32.3 us
  Pallas kernels  30.4 us (93%)
  local copies, waits for them, and re-layouts  1.26 us (4%)
  between operations  0.64 us (2%)
    pallas_call x1, Pallas kernels, per_device(): pl.pallas_call(functools.partial(kernel, regions, subs), out_shape=(pltpu...  30.4 us
    unnamed x2, local copies, waits for them, and re-layouts  1.26 us

profile of v3, /device:TPU:1, one launch (start us, length us, event | category | flops | bytes accessed | tf_op | source)
XLA Modules:
  0.0 32.3 jit_solution(16768923772698401847)
XLA Ops:
  0.6 30.4 %sph.1 = (f32[64,128]{1,0:T(8,128)S(1)}, f32[3,64,128]{2,1,0:T(8,128)S(1)}) custom-call(f32[3,64,128]{2,1,0:T(8,128)} %coords_hbm.1, f32[64,128]{1,0:T(8,128)} %smooth_hbm.1, f32[64,128]{1,0:T(8,128)} %masses_hbm.1, s32[1,64]{1,0:T(1,128)} %bitcast.4, s32[1,64]{1,0:T(1,128)} %bitcast.5, s32[4,64]{1,0:T(4,128)} %bitcast.3), custom_call_target="tpu_custom_call" | custom-call | tf_op jit(solution)/shard_map/sph/pallas_call | solution.py:326
  31.1 0.6 %copy.10 = f32[64,128]{1,0:T(8,128)} copy(f32[64,128]{1,0:T(8,128)S(1)} %get-tuple-element.2) | data formatting | bytes 65536
  31.7 0.6 %copy.11 = f32[3,64,128]{2,1,0:T(8,128)} copy(f32[3,64,128]{2,1,0:T(8,128)S(1)} %get-tuple-element.3) | data formatting | bytes 196608

commit v4 on v3

--- a/solution.py
+++ b/solution.py
@@ -19,6 +19,10 @@
 MESH = pl.DeviceIdType.MESH
 F32 = jnp.float32
 BF16 = jnp.bfloat16
+
+
+def largest(n, most=13):
+    return max(k for k in range(1, most + 1) if n % k == 0)
 
 
 def split3(v):
@@ -46,6 +50,15 @@
     down_earlier = run > 0
     up_earlier = run == last_run
 
+    def partner(k):
+        chips = regions // 2
+
+        def at(k):
+            y = k // 2
+            return 2 * (y if y < chips // 2 else chips + chips // 2 - 1 - y) + k % 2
+
+        return jnp.where(s == 0, 0 if k == regions - 1 else at(k + 1), at(k))
+
     def order(i):
         chips = regions // 2
         y = i // 2
@@ -53,8 +66,9 @@
         return jnp.where(s == 0, jnp.where(i == 0, regions - 1, place - 1), place)
 
     mine = order(r)
-    peers = [lax.rem(r + off, regions) for off in sorted(range(1, regions), key=lambda o: -min(o, regions - o))]
-    later = [order(p) > mine for p in peers]
+    peers = [partner(k) for k in range(regions)]
+    later = [mine < k for k in range(regions)]
+    earlier = [mine > k for k in range(regions)]
 
     def when_each(conditions, action):
         for n, condition in enumerate(conditions):
@@ -83,9 +97,8 @@
         pl.semaphore_wait(barrier, expected)
 
     def answer(n):
-        pl.semaphore_signal(ok, inc=1, device_id=(peers[n], s), device_id_type=MESH)
-
-    earlier = [jnp.logical_not(c) for c in later]
+        pl.semaphore_signal(ok.at[r], inc=1, device_id=(peers[n], s), device_id_type=MESH)
+
     when_each(earlier, answer)
 
     def answer_rim(n):
@@ -142,10 +155,6 @@
         send_meta(slot)
         send_rim(slot)
 
-    when_each(earlier, lambda n: copies[n].start())
-    when_each([up_earlier, down_earlier], send_meta)
-    landed[rim + r] = packed[r]
-
     def arrived(src):
         @pl.when(src != r)
         def _():
@@ -153,17 +162,45 @@
                 src_ref=packed.at[src], dst_ref=landed.at[rim + src], send_sem=send_sem.at[0],
                 recv_sem=recv_sem.at[src], device_id=(src, s), device_id_type=MESH).wait_recv()
 
-    @pl.when(mine < regions - 1)
+    def answered(n):
+        pl.semaphore_wait(ok.at[peers[n]], 1)
+        copies[n].start()
+
+    def send_up():
+        for src in last:
+            arrived(src)
+        send_rim(0)
+
+    top = RIM + tile_dev
+    last = range(regions - rim, regions)
+    def send_earlier(now):
+        for n in reversed(range(regions)):
+            pl.when(jnp.logical_and(earlier[n], now))(copies[n].start)
+
+    ahead = r >= regions - rim
+    send_earlier(ahead)
+    when_each([up_earlier, down_earlier], send_meta)
+    landed[rim + r] = packed[r]
+    when_each(later[: regions - 2], answered)
+    ends = jnp.logical_or(r < 2, r >= regions - 2)
+    pl.when(jnp.logical_and(up_earlier, ends))(send_up)
+    send_earlier(jnp.logical_not(ahead))
+    root = s == 0
+    pl.when(later[regions - 2])(functools.partial(answered, regions - 2))
+    pl.when(jnp.logical_and(later[regions - 1], jnp.logical_not(root)))(functools.partial(answered, regions - 1))
+    pl.when(jnp.logical_and(up_earlier, jnp.logical_not(ends)))(send_up)
+
+    @pl.when(jnp.logical_not(up_earlier))
     def _():
-        pl.semaphore_wait(ok, regions - 1 - mine)
-
-    when_each(later, lambda n: copies[n].start())
-    first = list(range(rim))
-    first += [g for g in range(regions - rim, regions) if g not in first]
-    for src in first:
-        arrived(src)
-    when_each([up_earlier, down_earlier], send_rim)
-    pl.when(jnp.logical_not(up_earlier))(functools.partial(answered_rim, 0))
+        for src in last:
+            arrived(src)
+        answered_rim(0)
+
+    @pl.when(down_earlier)
+    def _():
+        for src in range(rim):
+            arrived(src)
+        send_rim(1)
 
     lane = lax.broadcasted_iota(jnp.int32, (1, rows), 1)
     for load in loads[4:]:
@@ -174,9 +211,15 @@
         return carry
 
     lax.fori_loop(0, tile_dev, live_step, 0, unroll=UNROLL)
-    for src in range(regions):
-        if src not in first:
+    for src in range(rim, regions - rim):
+        arrived(src)
+
+    @pl.when(jnp.logical_not(down_earlier))
+    def _():
+        for src in range(1, rim):
             arrived(src)
+
+    pl.when(jnp.logical_and(later[regions - 1], root))(functools.partial(answered, regions - 1))
 
     def unpack(groups):
         for g in groups:
@@ -201,7 +244,7 @@
             partner_t[e] = jnp.concatenate([hi, mid, hi, mid, lo, hi], axis=0).T.astype(BF16)
             return carry
 
-        lax.fori_loop(a, b, partner_step, 0, unroll=UNROLL)
+        lax.fori_loop(a, b, partner_step, 0, unroll=largest(b - a))
 
     def density_of(e, partners, slot):
         hi, mid, lo = split3(own8[pl.ds(pl.multiple_of(e * 8, 8), 8), :])
@@ -237,7 +280,7 @@
             force_f[e] = jnp.concatenate([hi, v - hi], axis=0).astype(BF16)
             return carry
 
-        lax.fori_loop(a, b, step, 0, unroll=UNROLL)
+        lax.fori_loop(a, b, step, 0, unroll=largest(b - a))
 
     def force_of(t):
         feats = jnp.concatenate([force_f[p] for p in own_partners(t)], axis=1)
@@ -265,15 +308,18 @@
         force_of(t)
         return carry
 
-    top = RIM + tile_dev
-    unpack(range(rim, rim + regions))
-    pair_features(RIM, top)
-    lax.fori_loop(HALO, tile_dev - HALO, inner_density, 0, unroll=UNROLL)
-    force_features(RIM, top)
-    lax.fori_loop(RIM, tile_dev - RIM, inner_force, 0, unroll=UNROLL)
-    finish(RIM, tile_dev - RIM)
-
-    pl.when(jnp.logical_not(down_earlier))(functools.partial(answered_rim, 1))
+    unpack(range(rim + 1, rim + regions))
+    pair_features(RIM + group, top)
+    low = group + HALO
+    lax.fori_loop(low, tile_dev - HALO, inner_density, 0, unroll=largest(tile_dev - HALO - low))
+    force_features(RIM + low, top)
+    lax.fori_loop(low + HALO, tile_dev - RIM, inner_force, 0, unroll=largest(tile_dev - RIM - low - HALO))
+
+    @pl.when(jnp.logical_not(down_earlier))
+    def _():
+        arrived(0)
+        answered_rim(1)
+
 
     for copy in metas[0] + metas[1]:
         copy.wait_recv()
@@ -288,16 +334,20 @@
         live[top + k : top + k + 1, :] = (lane < rim_counts[1, 0, k]).astype(F32)
 
     rims[1].wait_recv()
-    unpack(range(rim + regions, 2 * rim + regions))
+    unpack([rim] + list(range(rim + regions, 2 * rim + regions)))
+    pair_features(RIM, RIM + group)
     pair_features(top, top + RIM)
+    for t in range(HALO, low):
+        density_of(RIM + t, own_partners(t), t)
     for k in range(HALO):
         density_of(top - HALO + k, own_partners(tile_dev - HALO + k), tile_dev - HALO + k)
         above = [rim_lists[1, nb, k] + (HALO + tile_dev) for nb in range(4)]
         density_of(top + k, above, None)
+    force_features(RIM + HALO, RIM + low)
     force_features(top - RIM, top + RIM)
-    for k in range(RIM):
-        force_of(tile_dev - RIM + k)
-    finish(tile_dev - RIM, tile_dev)
+    for t in list(range(RIM, low + HALO)) + list(range(tile_dev - RIM, tile_dev)):
+        force_of(t)
+    finish(RIM, tile_dev)
 
     rims[0].wait_recv()
     unpack(range(rim))
@@ -310,7 +360,8 @@
     for k in range(RIM):
         force_of(k)
     finish(0, RIM)
-    for copy in copies + metas[0] + metas[1] + rims:
+    when_each([mine != k for k in range(regions)], lambda n: copies[n].wait_send())
+    for copy in metas[0] + metas[1] + rims:
         copy.wait_send()
 
 
@@ -348,7 +399,7 @@
             pltpu.VMEM((ext, 16, rows), BF16),
             pltpu.VMEM((tile_dev * 8, rows), F32),
             dma((6,)), dma((regions,)), dma((regions,)), dma((2,)), dma((2,)), dma((4,)), dma((4,)), dma((2,)),
-            pltpu.SemaphoreType.REGULAR, pltpu.SemaphoreType.REGULAR((2,)),
+            pltpu.SemaphoreType.REGULAR((regions,)), pltpu.SemaphoreType.REGULAR((2,)),
         ],
         compiler_params=pltpu.CompilerParams(collective_id=0, has_side_effects=True),
         name="sph",

time: 32.6 us -> 31.4 us (0.963)
  Pallas kernels: 30.4 us -> 29.3 us
    pallas_call x1, Pallas kernels: 30.4 us -> 29.3 us  [per_device(): pl.pallas_call(functools.partial(kernel, regions, subs), out_shape=(pltpu...]
where the time goes in v4:
time: 31.4 us; the launch traced here: 31.2 us
  Pallas kernels  29.3 us (93%)
  local copies, waits for them, and re-layouts  1.26 us (4%)
  between operations  0.64 us (2%)
    pallas_call x1, Pallas kernels, per_device(): pl.pallas_call(functools.partial(kernel, regions, subs), out_shape=(pltpu...  29.3 us
    unnamed x2, local copies, waits for them, and re-layouts  1.26 us

profile of v4, /device:TPU:1, one launch (start us, length us, event | category | flops | bytes accessed | tf_op | source)
XLA Modules:
  0.0 31.2 jit_solution(6370046260444703315)
XLA Ops:
  0.6 29.3 %sph.1 = (f32[64,128]{1,0:T(8,128)S(1)}, f32[3,64,128]{2,1,0:T(8,128)S(1)}) custom-call(f32[3,64,128]{2,1,0:T(8,128)} %coords_hbm.1, f32[64,128]{1,0:T(8,128)} %smooth_hbm.1, f32[64,128]{1,0:T(8,128)} %masses_hbm.1, s32[1,64]{1,0:T(1,128)} %bitcast.4, s32[1,64]{1,0:T(1,128)} %bitcast.5, s32[4,64]{1,0:T(4,128)} %bitcast.3), custom_call_target="tpu_custom_call" | custom-call | tf_op jit(solution)/shard_map/sph/pallas_call | solution.py:377
  30.0 0.6 %copy.10 = f32[64,128]{1,0:T(8,128)} copy(f32[64,128]{1,0:T(8,128)S(1)} %get-tuple-element.2) | data formatting | bytes 65536
  30.6 0.6 %copy.11 = f32[3,64,128]{2,1,0:T(8,128)} copy(f32[3,64,128]{2,1,0:T(8,128)S(1)} %get-tuple-element.3) | data formatting | bytes 196608

commit v5 on v4

--- a/solution.py
+++ b/solution.py
@@ -12,6 +12,7 @@
 RIM = 2 * HALO
 FIELDS = 5
 UNROLL = 8
+DIRECT = 8
 SUB_RUN = 12
 LOG2E = math.log2(math.e)
 NORM_LOG2 = -1.5 * math.log2(math.pi)
@@ -36,7 +37,8 @@
            density_ref, accel_ref,
            coords, smooth, masses, owners, counts, lists, rim_counts_v, rim_lists_v, rim_counts, rim_lists,
            packed, landed, fields, live, partner8, own8, partner_t, weight_hi, weight_lo, raw, force8, force_f, sums8,
-           in_sem, send_sem, recv_sem, rim_send, rim_recv, meta_send, meta_recv, meta_sem, ok, rim_ok):
+           in_sem, send_sem, recv_sem, rim_send, rim_recv, meta_send, meta_recv, meta_sem, ok, rim_ok,
+           direct_send, direct_recv):
     tile_dev, rows = smooth.shape
     group = tile_dev // regions
     rim = RIM // group
@@ -85,12 +87,22 @@
         pl.semaphore_signal(barrier, inc=1, device_id=(r, (up, down)[n]), device_id_type=MESH)
 
     when_each([jnp.logical_not(up_earlier), jnp.logical_not(down_earlier)], greet_rim)
+    ahead = r >= regions - rim
+    gets_direct = jnp.logical_and(jnp.logical_not(down_earlier), r < DIRECT)
+    skips_rim = jnp.logical_and(up_earlier, r < DIRECT)
+    gives_direct = jnp.logical_and(up_earlier, ahead)
+
+    @pl.when(gets_direct)
+    def _():
+        for g in range(regions - rim, regions):
+            pl.semaphore_signal(barrier, inc=1, device_id=(g, down), device_id_type=MESH)
+
     loads = [pltpu.make_async_copy(src, dst, in_sem.at[n]) for n, (src, dst) in enumerate((
         (owners_hbm, owners), (coords_hbm, coords), (smooth_hbm, smooth), (masses_hbm, masses),
         (counts_hbm, counts), (lists_hbm, lists)))]
     for load in loads:
         load.start()
-    expected = mine + down_earlier.astype(jnp.int32) + up_earlier.astype(jnp.int32)
+    expected = mine + down_earlier.astype(jnp.int32) + up_earlier.astype(jnp.int32) + jnp.where(gives_direct, DIRECT, 0)
 
     @pl.when(expected > 0)
     def _():
@@ -169,7 +181,7 @@
     def send_up():
         for src in last:
             arrived(src)
-        send_rim(0)
+        pl.when(jnp.logical_not(skips_rim))(functools.partial(send_rim, 0))
 
     top = RIM + tile_dev
     last = range(regions - rim, regions)
@@ -177,7 +189,15 @@
         for n in reversed(range(regions)):
             pl.when(jnp.logical_and(earlier[n], now))(copies[n].start)
 
-    ahead = r >= regions - rim
+    direct = [pltpu.make_async_remote_copy(
+        src_ref=packed.at[d], dst_ref=landed.at[r - (regions - rim)], send_sem=direct_send.at[d],
+        recv_sem=direct_recv.at[r - (regions - rim)], device_id=(d, up), device_id_type=MESH) for d in range(DIRECT)]
+
+    @pl.when(gives_direct)
+    def _():
+        for copy in direct:
+            copy.start()
+
     send_earlier(ahead)
     when_each([up_earlier, down_earlier], send_meta)
     landed[rim + r] = packed[r]
@@ -349,7 +369,15 @@
         force_of(t)
     finish(RIM, tile_dev)
 
-    rims[0].wait_recv()
+    pl.when(jnp.logical_not(gets_direct))(rims[0].wait_recv)
+
+    @pl.when(gets_direct)
+    def _():
+        for g in range(rim):
+            pltpu.make_async_remote_copy(
+                src_ref=packed.at[g], dst_ref=landed.at[g], send_sem=direct_send.at[0],
+                recv_sem=direct_recv.at[g], device_id=(r, down), device_id_type=MESH).wait_recv()
+
     unpack(range(rim))
     pair_features(0, RIM)
     for k in range(HALO):
@@ -361,20 +389,36 @@
         force_of(k)
     finish(0, RIM)
     when_each([mine != k for k in range(regions)], lambda n: copies[n].wait_send())
-    for copy in metas[0] + metas[1] + rims:
+    pl.when(jnp.logical_not(skips_rim))(rims[0].wait_send)
+
+    @pl.when(gives_direct)
+    def _():
+        for copy in direct:
+            copy.wait_send()
+
+    for copy in metas[0] + metas[1] + rims[1:]:
         copy.wait_send()
+
+
+def store_kernel(density, accel, density_hbm, accel_hbm, sem):
+    copies = [pltpu.make_async_copy(density, density_hbm, sem.at[0]), pltpu.make_async_copy(accel, accel_hbm, sem.at[1])]
+    for copy in copies:
+        copy.start()
+    for copy in copies:
+        copy.wait()
 
 
 def per_device(coords, smooth, masses, owners, counts, neighbours):
     regions, subs = lax.axis_size("region"), lax.axis_size("sub")
     tile_dev, rows = smooth.shape
     group = tile_dev // regions
-    groups = regions + 2 * (RIM // group)
+    rim = RIM // group
+    groups = regions + 2 * rim
     ext = tile_dev + 2 * RIM
     owners, counts, lists = owners.reshape(1, -1), counts.reshape(1, -1), neighbours.T
     vmem = pl.BlockSpec(memory_space=pltpu.VMEM)
     dma = pltpu.SemaphoreType.DMA
-    return pl.pallas_call(
+    density, accel = pl.pallas_call(
         functools.partial(kernel, regions, subs),
         out_shape=(pltpu.VMEM((tile_dev, rows), F32), pltpu.VMEM((3, tile_dev, rows), F32)),
         in_specs=[pl.BlockSpec(memory_space=pl.ANY)] * 6,
@@ -400,10 +444,19 @@
             pltpu.VMEM((tile_dev * 8, rows), F32),
             dma((6,)), dma((regions,)), dma((regions,)), dma((2,)), dma((2,)), dma((4,)), dma((4,)), dma((2,)),
             pltpu.SemaphoreType.REGULAR((regions,)), pltpu.SemaphoreType.REGULAR((2,)),
+            dma((DIRECT,)), dma((rim,)),
         ],
         compiler_params=pltpu.CompilerParams(collective_id=0, has_side_effects=True),
         name="sph",
     )(coords, smooth, masses, owners, counts, lists)
+    return pl.pallas_call(
+        store_kernel,
+        out_shape=(jax.ShapeDtypeStruct(density.shape, F32), jax.ShapeDtypeStruct(accel.shape, F32)),
+        in_specs=[pl.BlockSpec(memory_space=pl.ANY)] * 2,
+        out_specs=[pl.BlockSpec(memory_space=pl.ANY)] * 2,
+        scratch_shapes=[dma((2,))],
+        name="store",
+    )(*(pltpu.with_memory_space_constraint(v, pltpu.VMEM) for v in (density, accel)))
 
 
 def solution(mesh):

time: 31.4 us -> 28.1 us (0.89)
  Pallas kernels: 29.3 us -> 27.3 us
  local copies, waits for them, and re-layouts: 1.26 us -> 0 us
    pallas_call x1, Pallas kernels: 29.3 us -> 26.6 us  [per_device(): pl.pallas_call(functools.partial(kernel, regions, subs), out_shape=(pltpu...]
    unnamed x2 -> x0, local copies, waits for them, and re-layouts: 1.26 us -> none
    pallas_call x0 -> x1, Pallas kernels: none -> 0.67 us  [per_device(): pl.pallas_call(store_kernel, out_shape=(jax.ShapeDtypeStruct(density.shap...]
where the time goes in v5:
time: 28.1 us; the launch traced here: 27.9 us
  Pallas kernels  27.3 us (97%)
  between operations  0.64 us (2%)
    pallas_call x1, Pallas kernels, per_device(): pl.pallas_call(functools.partial(kernel, regions, subs), out_shape=(pltpu...  26.6 us
    pallas_call x1, Pallas kernels, per_device(): pl.pallas_call(store_kernel, out_shape=(jax.ShapeDtypeStruct(density.shap...  0.67 us

profile of v5, /device:TPU:1, one launch (start us, length us, event | category | flops | bytes accessed | tf_op | source)
XLA Modules:
  0.0 27.9 jit_solution(15354363112944702224)
XLA Ops:
  0.6 26.6 %sph.1 = (f32[64,128]{1,0:T(8,128)S(1)}, f32[3,64,128]{2,1,0:T(8,128)S(1)}) custom-call(f32[3,64,128]{2,1,0:T(8,128)} %coords_hbm.1, f32[64,128]{1,0:T(8,128)} %smooth_hbm.1, f32[64,128]{1,0:T(8,128)} %masses_hbm.1, s32[1,64]{1,0:T(1,128)} %bitcast.4, s32[1,64]{1,0:T(1,128)} %bitcast.5, s32[4,64]{1,0:T(4,128)} %bitcast.3), custom_call_target="tpu_custom_call" | custom-call | tf_op jit(solution)/shard_map/sph/pallas_call | solution.py:421
  27.2 0.7 %store.1 = (f32[64,128]{1,0:T(8,128)}, f32[3,64,128]{2,1,0:T(8,128)}) custom-call(f32[64,128]{1,0:T(8,128)S(1)} %get-tuple-element.4.density, f32[3,64,128]{2,1,0:T(8,128)S(1)} %get-tuple-element.5.accel), custom_call_target="tpu_custom_call" | custom-call | tf_op jit(solution)/shard_map/store/pallas_call | solution.py:452

commit v6 on v5

--- a/solution.py
+++ b/solution.py
@@ -185,8 +185,8 @@
 
     top = RIM + tile_dev
     last = range(regions - rim, regions)
-    def send_earlier(now):
-        for n in reversed(range(regions)):
+    def send_earlier(now, ks):
+        for n in ks:
             pl.when(jnp.logical_and(earlier[n], now))(copies[n].start)
 
     direct = [pltpu.make_async_remote_copy(
@@ -198,13 +198,13 @@
         for copy in direct:
             copy.start()
 
-    send_earlier(ahead)
+    send_earlier(ahead, reversed(range(regions)))
     when_each([up_earlier, down_earlier], send_meta)
     landed[rim + r] = packed[r]
     when_each(later[: regions - 2], answered)
     ends = jnp.logical_or(r < 2, r >= regions - 2)
     pl.when(jnp.logical_and(up_earlier, ends))(send_up)
-    send_earlier(jnp.logical_not(ahead))
+    send_earlier(jnp.logical_not(ahead), range(regions))
     root = s == 0
     pl.when(later[regions - 2])(functools.partial(answered, regions - 2))
     pl.when(jnp.logical_and(later[regions - 1], jnp.logical_not(root)))(functools.partial(answered, regions - 1))
@@ -231,8 +231,10 @@
         return carry
 
     lax.fori_loop(0, tile_dev, live_step, 0, unroll=UNROLL)
+    middle = range(regions // 2, regions // 2 + 2)
     for src in range(rim, regions - rim):
-        arrived(src)
+        if src not in middle:
+            arrived(src)
 
     @pl.when(jnp.logical_not(down_earlier))
     def _():
@@ -328,10 +330,22 @@
         force_of(t)
         return carry
 
-    unpack(range(rim + 1, rim + regions))
-    pair_features(RIM + group, top)
     low = group + HALO
-    lax.fori_loop(low, tile_dev - HALO, inner_density, 0, unroll=largest(tile_dev - HALO - low))
+    gap = (group * middle[0], group * (middle[-1] + 1))
+    unpack([g for g in range(rim + 1, rim + regions) if g - rim not in middle])
+    pair_features(RIM + group, RIM + gap[0])
+    pair_features(RIM + gap[1], top)
+
+    def density_loop(a, b):
+        lax.fori_loop(a, b, inner_density, 0, unroll=largest(b - a))
+
+    density_loop(low, gap[0] - HALO)
+    density_loop(gap[1] + HALO, tile_dev - HALO)
+    for src in middle:
+        arrived(src)
+    unpack([rim + g for g in middle])
+    pair_features(RIM + gap[0], RIM + gap[1])
+    density_loop(gap[0] - HALO, gap[1] + HALO)
     force_features(RIM + low, top)
     lax.fori_loop(low + HALO, tile_dev - RIM, inner_force, 0, unroll=largest(tile_dev - RIM - low - HALO))
 

time: 28.1 us -> 28.1 us (level)
  no operation moved by 1% of the time
where the time goes in v6:
time: 28.1 us; the launch traced here: 27.9 us
  Pallas kernels  27.3 us (97%)
  between operations  0.64 us (2%)
    pallas_call x1, Pallas kernels, per_device(): pl.pallas_call(functools.partial(kernel, regions, subs), out_shape=(pltpu...  26.6 us
    pallas_call x1, Pallas kernels, per_device(): pl.pallas_call(store_kernel, out_shape=(jax.ShapeDtypeStruct(density.shap...  0.67 us

profile of v6, /device:TPU:1, one launch (start us, length us, event | category | flops | bytes accessed | tf_op | source)
XLA Modules:
  0.0 27.9 jit_solution(17292411379919186703)
XLA Ops:
  0.6 26.6 %sph.1 = (f32[64,128]{1,0:T(8,128)S(1)}, f32[3,64,128]{2,1,0:T(8,128)S(1)}) custom-call(f32[3,64,128]{2,1,0:T(8,128)} %coords_hbm.1, f32[64,128]{1,0:T(8,128)} %smooth_hbm.1, f32[64,128]{1,0:T(8,128)} %masses_hbm.1, s32[1,64]{1,0:T(1,128)} %bitcast.4, s32[1,64]{1,0:T(1,128)} %bitcast.5, s32[4,64]{1,0:T(4,128)} %bitcast.3), custom_call_target="tpu_custom_call" | custom-call | tf_op jit(solution)/shard_map/sph/pallas_call | solution.py:435
  27.2 0.7 %store.1 = (f32[64,128]{1,0:T(8,128)}, f32[3,64,128]{2,1,0:T(8,128)}) custom-call(f32[64,128]{1,0:T(8,128)S(1)} %get-tuple-element.4.density, f32[3,64,128]{2,1,0:T(8,128)S(1)} %get-tuple-element.5.accel), custom_call_target="tpu_custom_call" | custom-call | tf_op jit(solution)/shard_map/store/pallas_call | solution.py:466

commit v7 on v5

--- a/solution.py
+++ b/solution.py
@@ -195,8 +195,8 @@
 
     @pl.when(gives_direct)
     def _():
-        for copy in direct:
-            copy.start()
+        for d in [1] + list(range(DIRECT - 1, 1, -1)) + [0]:
+            direct[d].start()
 
     send_earlier(ahead)
     when_each([up_earlier, down_earlier], send_meta)

time: 28.1 us -> 28 us (level)
  Pallas kernels: 27.3 us -> 27 us
    pallas_call x1, Pallas kernels: 26.6 us -> 26.3 us  [per_device(): pl.pallas_call(functools.partial(kernel, regions, subs), out_shape=(pltpu...]
where the time goes in v7:
time: 28 us; the launch traced here: 27.6 us
  Pallas kernels  27 us (96%)
  between operations  0.64 us (2%)
    pallas_call x1, Pallas kernels, per_device(): pl.pallas_call(functools.partial(kernel, regions, subs), out_shape=(pltpu...  26.3 us
    pallas_call x1, Pallas kernels, per_device(): pl.pallas_call(store_kernel, out_shape=(jax.ShapeDtypeStruct(density.shap...  0.67 us

profile of v7, /device:TPU:1, one launch (start us, length us, event | category | flops | bytes accessed | tf_op | source)
XLA Modules:
  0.0 27.6 jit_solution(517663184960381654)
XLA Ops:
  0.6 26.3 %sph.1 = (f32[64,128]{1,0:T(8,128)S(1)}, f32[3,64,128]{2,1,0:T(8,128)S(1)}) custom-call(f32[3,64,128]{2,1,0:T(8,128)} %coords_hbm.1, f32[64,128]{1,0:T(8,128)} %smooth_hbm.1, f32[64,128]{1,0:T(8,128)} %masses_hbm.1, s32[1,64]{1,0:T(1,128)} %bitcast.4, s32[1,64]{1,0:T(1,128)} %bitcast.5, s32[4,64]{1,0:T(4,128)} %bitcast.3), custom_call_target="tpu_custom_call" | custom-call | tf_op jit(solution)/shard_map/sph/pallas_call | solution.py:421
  26.9 0.7 %store.1 = (f32[64,128]{1,0:T(8,128)}, f32[3,64,128]{2,1,0:T(8,128)}) custom-call(f32[64,128]{1,0:T(8,128)S(1)} %get-tuple-element.4.density, f32[3,64,128]{2,1,0:T(8,128)S(1)} %get-tuple-element.5.accel), custom_call_target="tpu_custom_call" | custom-call | tf_op jit(solution)/shard_map/store/pallas_call | solution.py:452
